TPU v7x, 256 devices: a whole 4x4x8 slice. The times are simulated.
256 devices in a mesh: row: 16 (over y, z_hi, core), col: 16 (over z_lo, x).
Axes of the slice: x: 4, y: 4, z: 8 (z_hi: 2, z_lo: 4; z = z_hi * 4 + z_lo), core: 2. Of those that a mesh axis runs over, the one named last changes fastest.
Arguments:
- fluid_data: float32 [51, 32768], P(None, ('row', 'col')), as said below
- center_data: float32 [51, 16384], P(None, ('col', 'row')), as said below
- poly_coef: float32 [48, 4], replicated, may hold values from -3 to 3
Outputs:
- fluid_motion: float32 [48, 32768], P(None, ('row', 'col'))
- center_load: float32 [48, 16384], P(None, ('col', 'row'))
Inputs may be any that keep to these rules, and one draw needn't show every extreme that they name: Rows 0 to 2 of fluid_data lie in [0, 1]; rows 3 and on are forces. Rows 0 and 1 of center_data lie in [0, 1] and row 2 lies in [-0.5, -0.02], so every center is at least 0.02 below every vertex; rows 3 and on are coefficients.
All inputs are finite; a program needn't handle non-finite values.
Results may differ from a plain program's by a relative error of at most 0.0003.
Values sent between devices are 32-bit elements; how exact they have to be, the bound alone decides.
No kernel may reach another device: no remote copies, remote signals or barrier semaphores. Data moves between devices by JAX's collectives and lax.ppermute only.
A program may use at most 64 MiB of HBM per device.

v0:
```python
import math

import jax
import jax.numpy as jnp
from jax import lax
from jax.sharding import PartitionSpec as P

WAVES = 64


def from_everyone(array, axis):
    devices = lax.axis_size(axis)
    return lax.all_to_all(
        jnp.broadcast_to(array[None], (devices, *array.shape)), axis, 0, 0, tiled=True
    )


def in_order(parts, dim):
    parts = jnp.moveaxis(parts, 0, dim)
    shape = parts.shape
    return parts.reshape(*shape[:dim], shape[dim] * shape[dim + 1], *shape[dim + 2 :])


def gather_directly(array, axis, dim):
    parts = from_everyone(array, axis)
    return in_order(parts, dim)


def split_up(array, dim, devices):
    before, after = (array.shape[:dim], array.shape[dim + 1 :])
    return jnp.moveaxis(array.reshape(*before, devices, -1, *after), dim, 0)


def sum_at_owner(array, axis, dim):
    parts = split_up(array, dim, lax.axis_size(axis))
    arrived = lax.all_to_all(parts, axis, split_axis=0, concat_axis=0, tiled=True)
    return arrived.sum(axis=0)


def kernel_block(center_pos, fluid_pos):
    dx = center_pos[0][:, None] - fluid_pos[0][None, :]
    dy = center_pos[1][:, None] - fluid_pos[1][None, :]
    dz = center_pos[2][:, None] - fluid_pos[2][None, :]
    sq = dx * dx + dy * dy + dz * dz
    phase = 2.0 * math.pi * WAVES * jnp.sqrt(sq)
    return jnp.sin(phase) / phase


def both_maps(centers, fluid):
    total = centers.shape[1]
    width = fluid.shape[1]
    block = math.gcd(total, max(128, 2**20 // width))
    count = total // block
    fluid_pos = fluid[:3]
    forces = fluid[3:]
    pieces = centers.reshape(centers.shape[0], count, block).transpose(1, 0, 2)

    def step(motion, piece):
        tile = kernel_block(piece[:3], fluid_pos)
        motion = motion + jnp.dot(
            piece[3:], tile, precision=lax.Precision.HIGHEST, preferred_element_type=jnp.float32
        )
        back = lax.dot_general(
            forces,
            tile,
            (((1,), (1,)), ((), ())),
            precision=lax.Precision.HIGHEST,
            preferred_element_type=jnp.float32,
        )
        return (motion, back)

    start = jnp.zeros((forces.shape[0], width), jnp.float32)
    motion, backs = lax.scan(step, start, pieces)
    loads = backs.transpose(1, 0, 2).reshape(forces.shape[0], total)
    return (motion, loads)


def per_device(fluid_data, center_data, poly_coef):
    fluid_block = gather_directly(fluid_data, "col", 1)
    center_block = gather_directly(center_data, "row", 1)
    partial_motion, partial_loads = both_maps(center_block, fluid_block)
    motion = sum_at_owner(partial_motion, "col", 1)
    loads = sum_at_owner(partial_loads, "row", 1)
    affine = poly_coef[:, 0:1] + jnp.dot(
        poly_coef[:, 1:],
        fluid_data[:3],
        precision=lax.Precision.HIGHEST,
        preferred_element_type=jnp.float32,
    )
    return (motion + affine, loads)


def solution(mesh):
    placed = (P(None, ("row", "col")), P(None, ("col", "row")), P())
    return jax.shard_map(
        per_device,
        mesh=mesh,
        in_specs=placed,
        out_specs=(P(None, ("row", "col")), P(None, ("col", "row"))),
        check_vma=False,
    )
```

profile of v0, /device:TPU:32, one launch (start us, length us, event | category | flops | bytes accessed | tf_op | source)
XLA Modules:
  0.0 172.9 jit_solution(15485215940686679854)
XLA Ops:
  0.6 0.8 broadcast_in_dim.24
  1.4 0.3 reshape.24
  1.7 23.8 %all_to_all.20 = f32[16,1,3264]{2,1,0:T(1,128)S(1)} all-to-all(f32[16,1,3264]{2,1,0:T(1,128)S(1)} %reshape.24), channel_id=1, replica_groups=mesh['row'=16,'col'=16] {'row'}, dimensions={0} | all-to-all | bytes 417792 | tf_op jit(solution)/shard_map/all_to_all | solution.py:13
  25.5 0.8 broadcast_in_dim.25
  26.3 6.2 %all-to-all-start.1 = ((f32[16,51,128]{2,1,0:T(8,128)}), f32[16,51,128]{2,1,0:T(8,128)S(1)}, u32[]{:S(2)}, u32[]{:S(2)}) async-start(f32[16,51,128]{2,1,0:T(8,128)} %broadcast_in_dim.25), calls=%async_computation.1 | async-start | bytes 917504 | tf_op jit(solution)/shard_map/all_to_all | solution.py:13
  32.6 0.5 broadcast.19
  33.1 1.1 reduce
  34.5 0.2 reshape_reshape.6
  34.7 11.2 %all-to-all-done.1 = f32[16,51,128]{2,1,0:T(8,128)S(1)} async-done(((f32[16,51,128]{2,1,0:T(8,128)}), f32[16,51,128]{2,1,0:T(8,128)S(1)}, u32[]{:S(2)}, u32[]{:S(2)}) %all-to-all-start.1) | async-done | bytes 417824 | tf_op jit(solution)/shard_map/all_to_all | solution.py:13
  45.9 91.1 %while.13 = (s32[]{:T(128)}, f32[48,2048]{1,0:T(8,128)S(1)}, f32[2,48,512]{2,1,0:T(8,128)S(1)}, f32[2,51,512]{2,0,1:T(2,128)S(1)}, f32[3,2048]{1,0:T(4,128)S(1)}...) while((s32[]{:T(128)}, f32[48,2048]{1,0:T(8,128)S(1)}, ...), condition=%wide.region_1.2_spmd.clone, body=%wide.region_0.1_spmd.clone.sunk | while | flops 1229127680 | bytes 1695923 | solution.py:73
  46.3 19.3 %convolution_add_fusion.3 = f32[48,2048]{1,0:T(8,128)S(1)} fusion(f32[2048]{0:T(1024)S(1)} %bitcast.67, f32[512]{0:T(512)S(1)} %bitcast.76, f32[2048]{0:T(1024)S(1)} %bitcast.69, f32[512]{0:T(512)S(1)} %bitcast.74, f32[2048]{0:T(1024)S(1)} %bitcast.65, f32[512]{0:T(512)S(1)} %bitcast.72, f32[48,2048]{1,0:T(8,128)S(1)} %get-tuple-element.155, ...), kind=kOutput, calls=%fused_computation.1.clone.1 | convolution fusion | flops 614662144 | bytes 915457 | tf_op jit(solution)/shard_map/while/body/eval_jaxpr/dot_general | solution.py:60
  65.6 20.2 %fusion.15 = f32[2,48,512]{2,1,0:T(8,128)S(1)} fusion(f32[2,48,512]{2,1,0:T(8,128)S(1)} %get-tuple-element.156, s32[]{:T(128)} %get-tuple-element.154, f32[48,2048]{1,0:T(8,128)S(1)} %get-tuple-element.170, f32[2048]{0:T(1024)S(1)} %bitcast.68, f32[512]{0:T(512)S(1)} %bitcast.77, f32[2048]{0:T(1024)S(1)} %bitcast.70, f32[512]{0:T(512)S(1)} %bitcast.75, ...), kind=kOutput, calls=%fused_computation.4.clone.1 | convolution fusion | flops 614465536 | bytes 522244 | tf_op jit(solution)/shard_map/while/body/eval_jaxpr/dot_general | solution.py:63
  90.8 19.0 %convolution_add_fusion.3 = f32[48,2048]{1,0:T(8,128)S(1)} fusion(f32[2048]{0:T(1024)S(1)} %bitcast.67, f32[512]{0:T(512)S(1)} %bitcast.76, f32[2048]{0:T(1024)S(1)} %bitcast.69, f32[512]{0:T(512)S(1)} %bitcast.74, f32[2048]{0:T(1024)S(1)} %bitcast.65, f32[512]{0:T(512)S(1)} %bitcast.72, f32[48,2048]{1,0:T(8,128)S(1)} %get-tuple-element.155, ...), kind=kOutput, calls=%fused_computation.1.clone.1 | convolution fusion | flops 614662144 | bytes 915457 | tf_op jit(solution)/shard_map/while/body/eval_jaxpr/dot_general | solution.py:60
  109.8 20.5 %fusion.15 = f32[2,48,512]{2,1,0:T(8,128)S(1)} fusion(f32[2,48,512]{2,1,0:T(8,128)S(1)} %get-tuple-element.156, s32[]{:T(128)} %get-tuple-element.154, f32[48,2048]{1,0:T(8,128)S(1)} %get-tuple-element.170, f32[2048]{0:T(1024)S(1)} %bitcast.68, f32[512]{0:T(512)S(1)} %bitcast.77, f32[2048]{0:T(1024)S(1)} %bitcast.70, f32[512]{0:T(512)S(1)} %bitcast.75, ...), kind=kOutput, calls=%fused_computation.4.clone.1 | convolution fusion | flops 614465536 | bytes 522244 | tf_op jit(solution)/shard_map/while/body/eval_jaxpr/dot_general | solution.py:63
  137.1 0.3 reshape_reshape.7
  137.5 0.9 reshape.26
  138.4 3.5 %all-to-all-start.3 = ((f32[16,1,3072]{2,1,0:T(1,128)}), f32[16,1,3072]{2,1,0:T(1,128)S(1)}, u32[]{:S(2)}, u32[]{:S(2)}) async-start(f32[16,1,3072]{2,1,0:T(1,128)} %reshape.26), calls=%async_computation.3 | async-start | bytes 393216 | tf_op jit(solution)/shard_map/all_to_all | solution.py:36
  142.0 0.9 copy.14
  142.9 12.4 %all-to-all-done.3 = f32[16,1,3072]{2,1,0:T(1,128)S(1)} async-done(((f32[16,1,3072]{2,1,0:T(1,128)}), f32[16,1,3072]{2,1,0:T(1,128)S(1)}, u32[]{:S(2)}, u32[]{:S(2)}) %all-to-all-start.3) | async-done | bytes 196640 | tf_op jit(solution)/shard_map/all_to_all | solution.py:36
  155.3 4.5 %all-to-all-start.2 = ((f32[16,48,128]{2,1,0:T(8,128)}), f32[16,48,128]{2,1,0:T(8,128)S(1)}, u32[]{:S(2)}, u32[]{:S(2)}) async-start(f32[16,48,128]{2,1,0:T(8,128)} %copy.14), calls=%async_computation.2 | async-start | bytes 786432 | tf_op jit(solution)/shard_map/all_to_all | solution.py:36
  159.8 1.1 reduce.1
  161.0 0.6 reduce_sum.19
  161.7 10.1 %all-to-all-done.2 = f32[16,48,128]{2,1,0:T(8,128)S(1)} async-done(((f32[16,48,128]{2,1,0:T(8,128)}), f32[16,48,128]{2,1,0:T(8,128)S(1)}, u32[]{:S(2)}, u32[]{:S(2)}) %all-to-all-start.2) | async-done | bytes 393248 | tf_op jit(solution)/shard_map/all_to_all | solution.py:36
  171.8 0.8 fusion.5
  (22 shorter events, 1.0 us)
Async XLA Ops:
  1.4 24.1 %copy-start = (f32[51,128]{1,0:T(8,128)S(1)}, f32[51,128]{1,0:T(8,128)}, u32[]{:S(2)}) copy-start(f32[51,128]{1,0:T(8,128)} %param.5) | copy-start | bytes 78340
  26.3 19.5 %all-to-all-start.1 = ((f32[16,51,128]{2,1,0:T(8,128)}), f32[16,51,128]{2,1,0:T(8,128)S(1)}, u32[]{:S(2)}, u32[]{:S(2)}) async-start(f32[16,51,128]{2,1,0:T(8,128)} %broadcast_in_dim.25), calls=%async_computation.1 | async-start | bytes 917504 | tf_op jit(solution)/shard_map/all_to_all | solution.py:13
  138.4 16.8 %all-to-all-start.3 = ((f32[16,1,3072]{2,1,0:T(1,128)}), f32[16,1,3072]{2,1,0:T(1,128)S(1)}, u32[]{:S(2)}, u32[]{:S(2)}) async-start(f32[16,1,3072]{2,1,0:T(1,128)} %reshape.26), calls=%async_computation.3 | async-start | bytes 393216 | tf_op jit(solution)/shard_map/all_to_all | solution.py:36
  142.9 16.9 %copy-start.1 = (f32[48,4]{0,1:T(4,128)S(1)}, f32[48,4]{0,1:T(4,128)}, u32[]{:S(2)}) copy-start(f32[48,4]{0,1:T(4,128)} %param.7) | copy-start | bytes 2308
  155.3 16.5 %all-to-all-start.2 = ((f32[16,48,128]{2,1,0:T(8,128)}), f32[16,48,128]{2,1,0:T(8,128)S(1)}, u32[]{:S(2)}, u32[]{:S(2)}) async-start(f32[16,48,128]{2,1,0:T(8,128)} %copy.14), calls=%async_computation.2 | async-start | bytes 786432 | tf_op jit(solution)/shard_map/all_to_all | solution.py:36
where the time goes:
time: 175 us; the launch traced here: 173 us
  matrix products  79.9 us (46%)
  waiting for transfers between devices  33.6 us (19%)
  blocking collectives  23.8 us (14%)
  starting transfers between devices  14.3 us (8%)
  loops' own time  11.8 us (7%)
  local copies, waits for them, and re-layouts  5.59 us (3%)
  other arithmetic  2.93 us (2%)
    dot_general x2, matrix products, step(): lax.dot_general(forces, tile, (((1,), (1,)), ((), ())), precision=lax.Pre...  40.7 us
    dot_general x2, matrix products, step(): jnp.dot(piece[3:], tile, precision=lax.Precision.HIGHEST, preferred_eleme...  38.3 us
    all_to_all x1, blocking collectives, from_everyone(): lax.all_to_all(jnp.broadcast_to(array[None], (devices, *array.shape)), ax...  23.8 us
    all_to_all x2, waiting for transfers between devices, sum_at_owner(): lax.all_to_all(parts, axis, split_axis=0, concat_axis=0, tiled=True)  22.4 us
    another operation x1, loops' own time, both_maps(): motion, backs = lax.scan(step, start, pieces)  11.8 us
    all_to_all x1, waiting for transfers between devices, from_everyone(): lax.all_to_all(jnp.broadcast_to(array[None], (devices, *array.shape)), ax...  11.2 us
    all_to_all x2, starting transfers between devices, sum_at_owner(): lax.all_to_all(parts, axis, split_axis=0, concat_axis=0, tiled=True)  8.04 us
    all_to_all x1, starting transfers between devices, from_everyone(): lax.all_to_all(jnp.broadcast_to(array[None], (devices, *array.shape)), ax...  6.23 us
  transfers between devices with their start and end apart: 3, of which 3 were waited for; matrix products, arithmetic and copies ran while one was open for 3% of the time, Pallas kernels for 0%

commit v1 on v0

v1 whole, which is shorter than its diff:
```python
import jax
import jax.numpy as jnp
from jax import lax
from jax.experimental import pallas as pl
from jax.experimental.pallas import tpu as pltpu
from jax.sharding import PartitionSpec as P

WAVES = 64
COLS = 48
LANES = 128
LEAD = -1.9530316595457846
TAIL = (-3.3578779781881196, 6.240606194702548, -6.649373004251278, 3.3689630874951395, -0.5120242670059871)

def tile_values(cx, cy, cz, fx, fy, fz):
    dx = cx - fx
    dy = cy - fy
    dz = cz - fz
    sq = dx * dx + dy * dy + dz * dz
    inv = lax.rsqrt(sq)
    turns = sq * inv
    rest = turns - jnp.round(turns)
    z = rest * rest
    p = z + TAIL[0]
    for c in TAIL[1:]:
        p = p * z + c
    return (rest * inv) * p

def split(a):
    hi = a.astype(jnp.bfloat16)
    lo = (a - hi.astype(jnp.float32)).astype(jnp.bfloat16)
    return hi, lo

def coupling_body(fluid, center, motion_out, load_out, cpos, cval, fval, fpos, t0, t1, acc, loads):
    nf = fluid.shape[0]
    nb = center.shape[0] // 2
    width = nf * LANES
    half = lax.broadcasted_iota(jnp.int32, (1, LANES), 1) < LANES // 2
    for k in range(nf):
        hi, lo = split(fluid[k, 0:COLS, :] * LEAD)
        fval[0:COLS, k * LANES:(k + 1) * LANES] = hi
        fval[COLS:2 * COLS, k * LANES:(k + 1) * LANES] = lo
        fpos[:, k * LANES:(k + 1) * LANES] = fluid[k, COLS:COLS + 3, :] * float(WAVES)
    for b in range(nb):
        one = center[2 * b]
        two = center[2 * b + 1]
        top = jnp.where(half, one, pltpu.roll(two, LANES // 2, 1))
        bot = jnp.where(half, pltpu.roll(one, LANES // 2, 1), two)
        val = jnp.concatenate([top[0:24], bot[0:24]], 0) * LEAD
        hi, lo = split(val)
        v = jnp.concatenate([hi, lo], 0)
        cval[b, :, 0:LANES] = v
        cval[b, :, LANES:2 * LANES] = v
        pos = jnp.concatenate([top[24:26], bot[24:25], jnp.zeros((5, LANES), jnp.float32)], 0) * float(WAVES)
        post = jnp.transpose(pos)
        for a in range(3):
            cpos[a, b * LANES:(b + 1) * LANES, :] = jnp.broadcast_to(post[:, a:a + 1], (LANES, LANES))

    acc[...] = jnp.zeros_like(acc)

    def compute(b, t):
        for k in range(nf):
            s = pl.ds(k * LANES, LANES)
            fx = fpos[0:1, s]; fy = fpos[1:2, s]; fz = fpos[2:3, s]
            for g in range(LANES // 16):
                rows = pl.ds(b * LANES + g * 16, 16)
                v = tile_values(cpos[0, rows, :], cpos[1, rows, :], cpos[2, rows, :], fx, fy, fz)
                hi, lo = split(v)
                t[g * 16:(g + 1) * 16, s] = hi
                t[LANES + g * 16:LANES + (g + 1) * 16, s] = lo

    def dots(b, t):
        acc[...] += jnp.dot(cval[b], t[...], preferred_element_type=jnp.float32)
        back = lax.dot_general(t[...], fval[...], (((1,), (1,)), ((), ())), preferred_element_type=jnp.float32)
        loads[pl.ds(b * LANES, LANES), :] = back[0:LANES, :] + back[LANES:2 * LANES, :]

    compute(0, t0)
    def pair(p, c):
        compute(2 * p + 1, t1)
        dots(2 * p, t0)
        compute(2 * p + 2, t0)
        dots(2 * p + 1, t1)
        return c
    lax.fori_loop(0, nb // 2 - 1, pair, 0)
    compute(nb - 1, t1)
    dots(nb - 2, t0)
    dots(nb - 1, t1)

    for k in range(nf):
        s = slice(k * LANES, (k + 1) * LANES)
        motion_out[k] = acc[0:COLS, s] + acc[COLS:2 * COLS, s]
    for b in range(nb):
        l = jnp.transpose(loads[b * LANES:(b + 1) * LANES, :])
        l = l[0:COLS] + l[COLS:2 * COLS]
        top = l[0:24]
        bot = l[24:48]
        load_out[2 * b] = jnp.where(half, top, pltpu.roll(bot, LANES // 2, 1))
        load_out[2 * b + 1] = jnp.where(half, pltpu.roll(top, LANES // 2, 1), bot)

def coupling(fluid, center):
    nf = fluid.shape[0]
    nc = center.shape[0]
    nb = nc // 2
    width = nf * LANES
    return pl.pallas_call(
        coupling_body,
        out_shape=(jax.ShapeDtypeStruct((nf, COLS, LANES), jnp.float32), jax.ShapeDtypeStruct((nc, 24, LANES), jnp.float32)),
        in_specs=[pl.BlockSpec(memory_space=pltpu.VMEM)] * 2,
        out_specs=(pl.BlockSpec(memory_space=pltpu.VMEM),) * 2,
        scratch_shapes=[
            pltpu.VMEM((3, nb * LANES, LANES), jnp.float32),
            pltpu.VMEM((nb, 2 * COLS, 2 * LANES), jnp.bfloat16),
            pltpu.VMEM((2 * COLS, width), jnp.bfloat16),
            pltpu.VMEM((3, width), jnp.float32),
            pltpu.VMEM((2 * LANES, width), jnp.bfloat16),
            pltpu.VMEM((2 * LANES, width), jnp.bfloat16),
            pltpu.VMEM((2 * COLS, width), jnp.float32),
            pltpu.VMEM((nb * LANES, 2 * COLS), jnp.float32),
        ],
        name="coupling",
    )(fluid, center)


def from_everyone(array, axis):
    devices = lax.axis_size(axis)
    return lax.all_to_all(jnp.broadcast_to(array[None], (devices, *array.shape)), axis, 0, 0, tiled=True)


def sum_at_owner(parts, axis):
    return lax.all_to_all(parts, axis, 0, 0, tiled=True).sum(axis=0)


def per_device(fluid_data, center_data, poly_coef):
    fluid = jnp.concatenate([fluid_data[3:], fluid_data[:3]], 0)
    places = jnp.concatenate([center_data[0:2], center_data[2:3], jnp.zeros_like(center_data[:1])], 0)
    center = jnp.concatenate(
        [
            jnp.concatenate([center_data[3:27], center_data[27:51]], 1),
            jnp.concatenate([places[0:2], places[2:4]], 1),
        ],
        0,
    )
    partial_motion, partial_loads = coupling(from_everyone(fluid, "col"), from_everyone(center, "row"))
    loads = sum_at_owner(partial_loads, "row")
    motion = sum_at_owner(partial_motion, "col")
    affine = poly_coef[:, 0:1] + jnp.dot(
        poly_coef[:, 1:],
        fluid_data[:3],
        precision=lax.Precision.HIGHEST,
        preferred_element_type=jnp.float32,
    )
    half = center_data.shape[1]
    return (motion + affine, jnp.concatenate([loads[:, :half], loads[:, half:]], 0))


def solution(mesh):
    placed = (P(None, ("row", "col")), P(None, ("col", "row")), P())
    return jax.shard_map(
        per_device,
        mesh=mesh,
        in_specs=placed,
        out_specs=(P(None, ("row", "col")), P(None, ("col", "row"))),
        check_vma=False,
    )
```

time: 175 us -> 95.9 us (0.55)
  matrix products: 79.9 us -> 0.84 us
  Pallas kernels: 0 us -> 13.5 us
  blocking collectives: 23.8 us -> 36.1 us
  loops' own time: 11.8 us -> 0 us
  waiting for transfers between devices: 33.6 us -> 25.2 us
  local copies, waits for them, and re-layouts: 5.59 us -> 3.04 us
  other arithmetic: 2.93 us -> 0.75 us
    dot_general x4 -> x0, matrix products: 79 us -> none  [the longest x2 40.7 us: step(): lax.dot_general(forces, tile, (((1,), (1,)), ((), ())), precision=lax.Pre...]
    all_to_all x0 -> x1, blocking collectives: none -> 16.8 us  [sum_at_owner(): return lax.all_to_all(parts, axis, 0, 0, tiled=True).sum(axis=0)]
    pallas_call x0 -> x1, Pallas kernels: none -> 13.5 us  [coupling(): pl.pallas_call(coupling_body, out_shape=(jax.ShapeDtypeStruct((nf, COLS,...]
    another operation x1 -> x0, loops' own time: 11.8 us -> none  [both_maps(): motion, backs = lax.scan(step, start, pieces)]
    all_to_all x2 -> x1, waiting for transfers between devices: 22.4 us -> 11.2 us  [sum_at_owner(): return lax.all_to_all(parts, axis, 0, 0, tiled=True).sum(axis=0)]
    all_to_all x1, blocking collectives: 23.8 us -> 19.3 us  [from_everyone(): lax.all_to_all(jnp.broadcast_to(array[None], (devices, *array.shape)), ax...]
    all_to_all x1, starting transfers between devices: 6.23 us -> 10.4 us  [from_everyone(): lax.all_to_all(jnp.broadcast_to(array[None], (devices, *array.shape)), ax...]
    all_to_all x2 -> x1, starting transfers between devices: 8.04 us -> 4.66 us  [sum_at_owner(): return lax.all_to_all(parts, axis, 0, 0, tiled=True).sum(axis=0)]
  transfers between devices with their start and end apart: 3 -> 2, of which waited for: 3 -> 2; matrix products, arithmetic and copies ran while one was open for 3% -> 1% of each run, Pallas kernels for 0% -> 0%
where the time goes in v1:
time: 95.9 us; the launch traced here: 95.3 us
  blocking collectives  36.1 us (38%)
  waiting for transfers between devices  25.2 us (26%)
  starting transfers between devices  15.1 us (16%)
  Pallas kernels  13.5 us (14%)
  local copies, waits for them, and re-layouts  3.04 us (3%)
    all_to_all x1, blocking collectives, from_everyone(): lax.all_to_all(jnp.broadcast_to(array[None], (devices, *array.shape)), ax...  19.3 us
    all_to_all x1, blocking collectives, sum_at_owner(): return lax.all_to_all(parts, axis, 0, 0, tiled=True).sum(axis=0)  16.8 us
    all_to_all x1, waiting for transfers between devices, from_everyone(): lax.all_to_all(jnp.broadcast_to(array[None], (devices, *array.shape)), ax...  14 us
    pallas_call x1, Pallas kernels, coupling(): pl.pallas_call(coupling_body, out_shape=(jax.ShapeDtypeStruct((nf, COLS,...  13.5 us
    all_to_all x1, waiting for transfers between devices, sum_at_owner(): return lax.all_to_all(parts, axis, 0, 0, tiled=True).sum(axis=0)  11.2 us
    all_to_all x1, starting transfers between devices, from_everyone(): lax.all_to_all(jnp.broadcast_to(array[None], (devices, *array.shape)), ax...  10.4 us
    all_to_all x1, starting transfers between devices, sum_at_owner(): return lax.all_to_all(parts, axis, 0, 0, tiled=True).sum(axis=0)  4.66 us
  transfers between devices with their start and end apart: 2, of which 2 were waited for; matrix products, arithmetic and copies ran while one was open for 1% of the time, Pallas kernels for 0%

profile of v1, /device:TPU:32, one launch (start us, length us, event | category | flops | bytes accessed | tf_op | source)
XLA Modules:
  0.0 95.3 jit_solution(7585734955538784486)
XLA Ops:
  0.6 0.0 copy-start.2
  0.6 0.8 fusion.5
  1.5 0.0 copy-done.2
  1.5 0.0 slice-start.1
  1.5 0.7 slice-done.1
  2.2 0.1 fusion.1
  2.2 0.7 broadcast_in_dim.5
  3.0 0.0 copy-start.1
  3.0 10.4 %all-to-all-start.1 = ((f32[16,26,128]{2,1,0:T(8,128)}), f32[16,26,128]{2,1,0:T(8,128)S(1)}, u32[]{:S(2)}, u32[]{:S(2)}) async-start(f32[16,26,128]{2,1,0:T(8,128)} %broadcast_in_dim.5), calls=%async_computation.1 | async-start | bytes 524288 | tf_op jit(solution)/shard_map/all_to_all | solution.py:125
  13.4 0.0 copy-done.1
  13.4 0.0 slice-start
  13.4 0.7 slice-done
  14.1 14.0 %all-to-all-done.1.center = f32[16,26,128]{2,1,0:T(8,128)S(1)} async-done(((f32[16,26,128]{2,1,0:T(8,128)}), f32[16,26,128]{2,1,0:T(8,128)S(1)}, u32[]{:S(2)}, u32[]{:S(2)}) %all-to-all-start.1) | async-done | bytes 213024 | tf_op jit(solution)/shard_map/all_to_all | solution.py:125
  28.1 0.0 copy-start
  28.2 19.3 %all_to_all.20.fluid = f32[16,51,128]{2,1,0:T(8,128)} all-to-all(f32[16,51,128]{2,1,0:T(8,128)S(1)} %broadcast_in_dim.4), channel_id=1, replica_groups=mesh['row'=16,'col'=16] {'col'}, dimensions={0} | all-to-all | bytes 835584 | tf_op jit(solution)/shard_map/all_to_all | solution.py:125
  47.5 0.0 copy-done
  47.5 13.5 %coupling.1 = (f32[16,48,128]{2,1,0:T(8,128)}, f32[16,24,128]{2,1,0:T(8,128)}) custom-call(f32[16,51,128]{2,1,0:T(8,128)} %all_to_all.20.fluid, f32[16,26,128]{2,1,0:T(8,128)} %copy-done), custom_call_target="tpu_custom_call" | custom-call | tf_op jit(solution)/shard_map/coupling/pallas_call | solution.py:104
  61.0 16.8 %all_to_all.21 = f32[16,24,128]{2,1,0:T(8,128)S(1)} all-to-all(f32[16,24,128]{2,1,0:T(8,128)} %get-tuple-element.5), channel_id=1, replica_groups=mesh['row'=16,'col'=16] {'row'}, dimensions={0} | all-to-all | bytes 393216 | tf_op jit(solution)/shard_map/all_to_all | solution.py:129
  77.8 4.7 %all-to-all-start.2 = ((f32[16,48,128]{2,1,0:T(8,128)}), f32[16,48,128]{2,1,0:T(8,128)S(1)}, u32[]{:S(2)}, u32[]{:S(2)}) async-start(f32[16,48,128]{2,1,0:T(8,128)} %get-tuple-element.4), calls=%async_computation.2 | async-start | bytes 786432 | tf_op jit(solution)/shard_map/all_to_all | solution.py:129
  82.5 0.0 copy-done.3
  82.5 0.1 fusion.6
  82.6 0.6 pad_maximum_fusion.1
  83.2 11.2 %all-to-all-done.2 = f32[16,48,128]{2,1,0:T(8,128)S(1)} async-done(((f32[16,48,128]{2,1,0:T(8,128)}), f32[16,48,128]{2,1,0:T(8,128)S(1)}, u32[]{:S(2)}, u32[]{:S(2)}) %all-to-all-start.2) | async-done | bytes 393248 | tf_op jit(solution)/shard_map/all_to_all | solution.py:129
  94.5 0.8 fusion
  (8 shorter events, 0.1 us)
Async XLA Ops:
  0.6 0.8 copy-start.2
  1.5 0.7 slice-start.1
  3.0 10.4 %copy-start.1 = (f32[51,128]{1,0:T(8,128)S(1)}, f32[51,128]{1,0:T(8,128)}, u32[]{:S(2)}) copy-start(f32[51,128]{1,0:T(8,128)} %param.3) | copy-start | bytes 78340
  3.0 25.2 %all-to-all-start.1 = ((f32[16,26,128]{2,1,0:T(8,128)}), f32[16,26,128]{2,1,0:T(8,128)S(1)}, u32[]{:S(2)}, u32[]{:S(2)}) async-start(f32[16,26,128]{2,1,0:T(8,128)} %broadcast_in_dim.5), calls=%async_computation.1 | async-start | bytes 524288 | tf_op jit(solution)/shard_map/all_to_all | solution.py:125
  13.4 0.7 slice-start
  28.1 19.3 %copy-start = (f32[16,26,128]{2,1,0:T(8,128)}, f32[16,26,128]{2,1,0:T(8,128)S(1)}, u32[]{:S(2)}) copy-start(f32[16,26,128]{2,1,0:T(8,128)S(1)} %all-to-all-done.1.center) | copy-start | bytes 638980
  77.8 4.7 %copy-start.3 = (f32[48,4]{0,1:T(4,128)S(1)}, f32[48,4]{0,1:T(4,128)}, u32[]{:S(2)}) copy-start(f32[48,4]{0,1:T(4,128)} %param.5) | copy-start | bytes 2308
  77.8 16.6 %all-to-all-start.2 = ((f32[16,48,128]{2,1,0:T(8,128)}), f32[16,48,128]{2,1,0:T(8,128)S(1)}, u32[]{:S(2)}, u32[]{:S(2)}) async-start(f32[16,48,128]{2,1,0:T(8,128)} %get-tuple-element.4), calls=%async_computation.2 | async-start | bytes 786432 | tf_op jit(solution)/shard_map/all_to_all | solution.py:129

commit v2 on v1

--- a/solution.py
+++ b/solution.py
@@ -30,19 +30,23 @@
     lo = (a - hi.astype(jnp.float32)).astype(jnp.bfloat16)
     return hi, lo
 
-def coupling_body(fluid, center, motion_out, load_out, cpos, cval, fval, fpos, t0, t1, acc, loads):
-    nf = fluid.shape[0]
-    nb = center.shape[0] // 2
+def coupling_body(fluid_a, fluid_b, center_a, center_b, motion_a, motion_b, load_a, load_b, cpos, cval, fval, fpos, t0, t1, acc, loads):
+    hf = fluid_a.shape[0]
+    nf = 2 * hf
+    hb = center_a.shape[0] // 2
+    nb = 2 * hb
     width = nf * LANES
     half = lax.broadcasted_iota(jnp.int32, (1, LANES), 1) < LANES // 2
     for k in range(nf):
-        hi, lo = split(fluid[k, 0:COLS, :] * LEAD)
+        chunk = (fluid_a, fluid_b)[k // hf].at[k % hf]
+        hi, lo = split(chunk[0:COLS, :] * LEAD)
         fval[0:COLS, k * LANES:(k + 1) * LANES] = hi
         fval[COLS:2 * COLS, k * LANES:(k + 1) * LANES] = lo
-        fpos[:, k * LANES:(k + 1) * LANES] = fluid[k, COLS:COLS + 3, :] * float(WAVES)
+        fpos[:, k * LANES:(k + 1) * LANES] = chunk[COLS:COLS + 3, :] * float(WAVES)
     for b in range(nb):
-        one = center[2 * b]
-        two = center[2 * b + 1]
+        side = (center_a, center_b)[b // hb]
+        one = side[2 * (b % hb)]
+        two = side[2 * (b % hb) + 1]
         top = jnp.where(half, one, pltpu.roll(two, LANES // 2, 1))
         bot = jnp.where(half, pltpu.roll(one, LANES // 2, 1), two)
         val = jnp.concatenate([top[0:24], bot[0:24]], 0) * LEAD
@@ -87,25 +91,28 @@
 
     for k in range(nf):
         s = slice(k * LANES, (k + 1) * LANES)
-        motion_out[k] = acc[0:COLS, s] + acc[COLS:2 * COLS, s]
+        (motion_a, motion_b)[k // hf][k % hf] = acc[0:COLS, s] + acc[COLS:2 * COLS, s]
     for b in range(nb):
         l = jnp.transpose(loads[b * LANES:(b + 1) * LANES, :])
         l = l[0:COLS] + l[COLS:2 * COLS]
         top = l[0:24]
         bot = l[24:48]
-        load_out[2 * b] = jnp.where(half, top, pltpu.roll(bot, LANES // 2, 1))
-        load_out[2 * b + 1] = jnp.where(half, pltpu.roll(top, LANES // 2, 1), bot)
-
-def coupling(fluid, center):
-    nf = fluid.shape[0]
-    nc = center.shape[0]
-    nb = nc // 2
-    width = nf * LANES
+        side = (load_a, load_b)[b // hb]
+        side[2 * (b % hb)] = jnp.where(half, top, pltpu.roll(bot, LANES // 2, 1))
+        side[2 * (b % hb) + 1] = jnp.where(half, pltpu.roll(top, LANES // 2, 1), bot)
+
+def coupling(fluid_a, fluid_b, center_a, center_b):
+    hf = fluid_a.shape[0]
+    hc = center_a.shape[0]
+    nb = hc
+    width = 2 * hf * LANES
+    motion = jax.ShapeDtypeStruct((hf, COLS, LANES), jnp.float32)
+    load = jax.ShapeDtypeStruct((hc, COLS // 2, LANES), jnp.float32)
     return pl.pallas_call(
         coupling_body,
-        out_shape=(jax.ShapeDtypeStruct((nf, COLS, LANES), jnp.float32), jax.ShapeDtypeStruct((nc, 24, LANES), jnp.float32)),
-        in_specs=[pl.BlockSpec(memory_space=pltpu.VMEM)] * 2,
-        out_specs=(pl.BlockSpec(memory_space=pltpu.VMEM),) * 2,
+        out_shape=(motion, motion, load, load),
+        in_specs=[pl.BlockSpec(memory_space=pltpu.VMEM)] * 4,
+        out_specs=(pl.BlockSpec(memory_space=pltpu.VMEM),) * 4,
         scratch_shapes=[
             pltpu.VMEM((3, nb * LANES, LANES), jnp.float32),
             pltpu.VMEM((nb, 2 * COLS, 2 * LANES), jnp.bfloat16),
@@ -117,16 +124,51 @@
             pltpu.VMEM((nb * LANES, 2 * COLS), jnp.float32),
         ],
         name="coupling",
-    )(fluid, center)
-
-
-def from_everyone(array, axis):
-    devices = lax.axis_size(axis)
-    return lax.all_to_all(jnp.broadcast_to(array[None], (devices, *array.shape)), axis, 0, 0, tiled=True)
-
-
-def sum_at_owner(parts, axis):
-    return lax.all_to_all(parts, axis, 0, 0, tiled=True).sum(axis=0)
+    )(fluid_a, fluid_b, center_a, center_b)
+
+
+AXES = ("row", "col")
+
+
+def place(x, y, z, core):
+    return (y * 4 + (z // 4) * 2 + core) * 16 + (z % 4) * 4 + x
+
+
+def partners(move):
+    spots = [(x, y, z, c) for x in range(4) for y in range(4) for z in range(8) for c in range(2)]
+    return [(place(*spot), place(*move(*spot))) for spot in spots]
+
+
+def near(v):
+    return v ^ 1
+
+
+def wrap(v):
+    return 3 - v
+
+
+FLUID_STAGES = (
+    partners(lambda x, y, z, c: (near(x), y, z, c)),
+    partners(lambda x, y, z, c: (wrap(x), y, z, c)),
+    partners(lambda x, y, z, c: (x, y, z ^ 1, c)),
+    partners(lambda x, y, z, c: (x, y, z, 1 - c)),
+)
+CENTER_STAGES = (
+    partners(lambda x, y, z, c: (x, y, 2 * near(z // 2) + z % 2, c)),
+    partners(lambda x, y, z, c: (x, y, 2 * wrap(z // 2) + z % 2, c)),
+    partners(lambda x, y, z, c: (x, near(y), z, c)),
+    partners(lambda x, y, z, c: (x, wrap(y), z, c)),
+)
+
+
+def gather_step(held, stage):
+    return held, lax.ppermute(held, AXES, stage)
+
+
+def sum_step(mine, theirs, stage):
+    arrived = lax.ppermute(theirs, AXES, stage)
+    half = mine.shape[0] // 2
+    return mine[:half] + arrived[:half], mine[half:] + arrived[half:]
 
 
 def per_device(fluid_data, center_data, poly_coef):
@@ -139,9 +181,21 @@
         ],
         0,
     )
-    partial_motion, partial_loads = coupling(from_everyone(fluid, "col"), from_everyone(center, "row"))
-    loads = sum_at_owner(partial_loads, "row")
-    motion = sum_at_owner(partial_motion, "col")
+    fluid = fluid[None]
+    center = center[None]
+    fluids = (fluid, None)
+    centers = (center, None)
+    for i in range(4):
+        held = fluids[0] if i == 0 else jnp.concatenate(fluids, 0)
+        fluids = gather_step(held, FLUID_STAGES[i])
+        held = centers[0] if i == 0 else jnp.concatenate(centers, 0)
+        centers = gather_step(held, CENTER_STAGES[i])
+    motion, motion_away, loads, loads_away = coupling(*fluids, *centers)
+    for i in (3, 2, 1):
+        motion, motion_away = sum_step(motion, motion_away, FLUID_STAGES[i])
+        loads, loads_away = sum_step(loads, loads_away, CENTER_STAGES[i])
+    motion = (motion + lax.ppermute(motion_away, AXES, FLUID_STAGES[0]))[0]
+    loads = (loads + lax.ppermute(loads_away, AXES, CENTER_STAGES[0]))[0]
     affine = poly_coef[:, 0:1] + jnp.dot(
         poly_coef[:, 1:],
         fluid_data[:3],

time: 95.9 us -> 76.4 us (0.80)
  blocking collectives: 36.1 us -> 0 us
  starting transfers between devices: 15.1 us -> 29.6 us
  other arithmetic: 0.75 us -> 2.3 us
    all_to_all x2 -> x0, blocking collectives: 36.1 us -> none  [the longest x1 19.3 us: from_everyone(): lax.all_to_all(jnp.broadcast_to(array[None], (devices, *array.shape)), ax...]
    ppermute x0 -> x16, starting transfers between devices: none -> 29.6 us  [the longest x8 17.4 us: gather_step(): return (held, lax.ppermute(held, AXES, stage))]
    ppermute x0 -> x16, waiting for transfers between devices: none -> 26 us  [the longest x6 14.2 us: sum_step(): arrived = lax.ppermute(theirs, AXES, stage)]
    all_to_all x2 -> x0, waiting for transfers between devices: 25.2 us -> none  [the longest x1 14 us: from_everyone(): lax.all_to_all(jnp.broadcast_to(array[None], (devices, *array.shape)), ax...]
    all_to_all x2 -> x0, starting transfers between devices: 15.1 us -> none  [the longest x1 10.4 us: from_everyone(): lax.all_to_all(jnp.broadcast_to(array[None], (devices, *array.shape)), ax...]
    add x0 -> x7, other arithmetic: none -> 1.55 us  [the longest x6 0.93 us: sum_step(): return (mine[:half] + arrived[:half], mine[half:] + arrived[half:])]
    unnamed x8 -> x18, local copies, waits for them, and re-layouts: 0.02 us -> 1.35 us
  transfers between devices with their start and end apart: 2 -> 16, of which waited for: 2 -> 11; matrix products, arithmetic and copies ran while one was open for 1% -> 1% of each run, Pallas kernels for 0% -> 0%
where the time goes in v2:
time: 76.4 us; the launch traced here: 76 us
  starting transfers between devices  29.6 us (39%)
  waiting for transfers between devices  26 us (34%)
  Pallas kernels  13.6 us (18%)
  local copies, waits for them, and re-layouts  3.54 us (5%)
  other arithmetic  2.3 us (3%)
  between operations  0.79 us (1%)
    ppermute x8, starting transfers between devices, gather_step(): return (held, lax.ppermute(held, AXES, stage))  17.4 us
    ppermute x6, waiting for transfers between devices, sum_step(): arrived = lax.ppermute(theirs, AXES, stage)  14.2 us
    pallas_call x1, Pallas kernels, coupling(): pl.pallas_call(coupling_body, out_shape=(motion, motion, load, load), in_...  13.6 us
    ppermute x6, starting transfers between devices, sum_step(): arrived = lax.ppermute(theirs, AXES, stage)  9.93 us
    ppermute x8, waiting for transfers between devices, gather_step(): return (held, lax.ppermute(held, AXES, stage))  6.61 us
    ppermute x1, waiting for transfers between devices, per_device(): motion = (motion + lax.ppermute(motion_away, AXES, FLUID_STAGES[0]))[0]  3.21 us
    ppermute x1, starting transfers between devices, per_device(): loads = (loads + lax.ppermute(loads_away, AXES, CENTER_STAGES[0]))[0]  2.22 us
    ppermute x1, waiting for transfers between devices, per_device(): loads = (loads + lax.ppermute(loads_away, AXES, CENTER_STAGES[0]))[0]  2.01 us
  transfers between devices with their start and end apart: 16, of which 11 were waited for; matrix products, arithmetic and copies ran while one was open for 1% of the time, Pallas kernels for 0%

profile of v2, /device:TPU:32, one launch (start us, length us, event | category | flops | bytes accessed | tf_op | source)
XLA Modules:
  0.0 76.0 jit_solution(9563325528080120572)
XLA Ops:
  2.1 1.5 %collective-permute-start = (f32[1,51,128]{2,1,0:T(8,128)S(1)}, f32[1,51,128]{2,1,0:T(8,128)S(1)}, u32[]{:S(2)}, u32[]{:S(2)}) collective-permute-start(f32[1,51,128]{2,1,0:T(8,128)S(1)} %maximum_bitcast_fusion), channel_id=1, source_target_pairs={{0,1},{16,17},{4,5},{20,21},{8,9},{24,25},{12,13},{28,29},{32,33},... | collective-permute-start | bytes 78344 | tf_op jit(solution)/shard_map/ppermute | solution.py:165
  4.3 3.3 %collective-permute-start.4 = (f32[1,26,128]{2,1,0:T(8,128)S(1)}, f32[1,26,128]{2,1,0:T(8,128)S(1)}, u32[]{:S(2)}, u32[]{:S(2)}) collective-permute-start(f32[1,26,128]{2,1,0:T(8,128)S(1)} %fusion.4), channel_id=1, source_target_pairs={{0,8},{16,24},{4,12},{20,28},{8,0},{24,16},{12,4},{28,20},{32,40},... | collective-permute-start | bytes 39944 | tf_op jit(solution)/shard_map/ppermute | solution.py:165
  7.7 2.2 %collective-permute-start.1 = (f32[2,51,128]{2,1,0:T(8,128)S(1)}, f32[2,51,128]{2,1,0:T(8,128)S(1)}, u32[]{:S(2)}, u32[]{:S(2)}) collective-permute-start(f32[2,51,128]{2,1,0:T(8,128)S(1)} %pad_maximum_fusion.4), channel_id=1, source_target_pairs={{0,3},{16,19},{4,7},{20,23},{8,11},{24,27},{12,15},{28,31},{32,35}... | collective-permute-start | bytes 156680 | tf_op jit(solution)/shard_map/ppermute | solution.py:165
  9.8 4.6 %collective-permute-start.5 = (f32[2,26,128]{2,1,0:T(8,128)S(1)}, f32[2,26,128]{2,1,0:T(8,128)S(1)}, u32[]{:S(2)}, u32[]{:S(2)}) collective-permute-start(f32[2,26,128]{2,1,0:T(8,128)S(1)} %pad_maximum_fusion.5), channel_id=1, source_target_pairs={{0,40},{16,56},{4,44},{20,60},{8,32},{24,48},{12,36},{28,52},{32,8... | collective-permute-start | bytes 79880 | tf_op jit(solution)/shard_map/ppermute | solution.py:165
  14.4 1.1 %collective-permute-start.2 = (f32[4,51,128]{2,1,0:T(8,128)S(1)}, f32[4,51,128]{2,1,0:T(8,128)S(1)}, u32[]{:S(2)}, u32[]{:S(2)}) collective-permute-start(f32[4,51,128]{2,1,0:T(8,128)S(1)} %pad_maximum_fusion.2), channel_id=1, source_target_pairs={{0,4},{16,20},{4,0},{20,16},{8,12},{24,28},{12,8},{28,24},{32,36},... | collective-permute-start | bytes 313352 | tf_op jit(solution)/shard_map/ppermute | solution.py:165
  15.5 0.9 %collective-permute-done.5 = f32[2,26,128]{2,1,0:T(8,128)S(1)} collective-permute-done((f32[2,26,128]{2,1,0:T(8,128)S(1)}, f32[2,26,128]{2,1,0:T(8,128)S(1)}, u32[]{:S(2)}, u32[]{:S(2)}) %collective-permute-start.5) | collective-permute-done | bytes 26656 | tf_op jit(solution)/shard_map/ppermute | solution.py:165
  16.4 1.6 %collective-permute-start.6 = (f32[4,26,128]{2,1,0:T(8,128)S(1)}, f32[4,26,128]{2,1,0:T(8,128)S(1)}, u32[]{:S(2)}, u32[]{:S(2)}) collective-permute-start(f32[4,26,128]{2,1,0:T(8,128)S(1)} %pad_maximum_fusion.3), channel_id=1, source_target_pairs={{0,64},{16,80},{4,68},{20,84},{8,72},{24,88},{12,76},{28,92},{32,9... | collective-permute-start | bytes 159752 | tf_op jit(solution)/shard_map/ppermute | solution.py:165
  18.0 1.3 %collective-permute-done.2 = f32[4,51,128]{2,1,0:T(8,128)S(1)} collective-permute-done((f32[4,51,128]{2,1,0:T(8,128)S(1)}, f32[4,51,128]{2,1,0:T(8,128)S(1)}, u32[]{:S(2)}, u32[]{:S(2)}) %collective-permute-start.2) | collective-permute-done | bytes 104480 | tf_op jit(solution)/shard_map/ppermute | solution.py:165
  19.4 1.2 %collective-permute-done.6 = f32[4,26,128]{2,1,0:T(8,128)S(1)} collective-permute-done((f32[4,26,128]{2,1,0:T(8,128)S(1)}, f32[4,26,128]{2,1,0:T(8,128)S(1)}, u32[]{:S(2)}, u32[]{:S(2)}) %collective-permute-start.6) | collective-permute-done | bytes 53280 | tf_op jit(solution)/shard_map/ppermute | solution.py:165
  20.7 3.1 %collective-permute-start.7 = (f32[8,26,128]{2,1,0:T(8,128)S(1)}, f32[8,26,128]{2,1,0:T(8,128)S(1)}, u32[]{:S(2)}, u32[]{:S(2)}) collective-permute-start(f32[8,26,128]{2,1,0:T(8,128)S(1)} %pad_maximum_fusion.1.center_a), channel_id=1, source_target_pairs={{0,192},{16,208},{4,196},{20,212},{8,200},{24,216},{12,204},{28,22... | collective-permute-start | bytes 319496 | tf_op jit(solution)/shard_map/ppermute | solution.py:165
  23.8 3.2 %collective-permute-done.7.center_b = f32[8,26,128]{2,1,0:T(8,128)S(1)} collective-permute-done((f32[8,26,128]{2,1,0:T(8,128)S(1)}, f32[8,26,128]{2,1,0:T(8,128)S(1)}, u32[]{:S(2)}, u32[]{:S(2)}) %collective-permute-start.7) | collective-permute-done | bytes 106528 | tf_op jit(solution)/shard_map/ppermute | solution.py:165
  28.3 13.6 %coupling.1 = (f32[8,48,128]{2,1,0:T(8,128)}, f32[8,48,128]{2,1,0:T(8,128)}, f32[8,24,128]{2,1,0:T(8,128)}, f32[8,24,128]{2,1,0:T(8,128)}) custom-call(f32[8,51,128]{2,1,0:T(8,128)} %copy-done, f32[8,51,128]{2,1,0:T(8,128)} %copy-done.2, f32[8,26,128]{2,1,0:T(8,128)} %copy-done.1, f32[8,26,128]{2,1,0:T(8,128)} %copy-done.4), custom_call_target="tpu_custom_call" | custom-call | tf_op jit(solution)/shard_map/coupling/pallas_call | solution.py:111
  41.9 3.0 %collective-permute-start.12 = (f32[8,24,128]{2,1,0:T(8,128)}, f32[8,24,128]{2,1,0:T(8,128)S(1)}, u32[]{:S(2)}, u32[]{:S(2)}) collective-permute-start(f32[8,24,128]{2,1,0:T(8,128)} %get-tuple-element.9), channel_id=1, source_target_pairs={{0,192},{16,208},{4,196},{20,212},{8,200},{24,216},{12,204},{28,22... | collective-permute-start | bytes 294920 | tf_op jit(solution)/shard_map/ppermute | solution.py:169
  44.9 3.0 %collective-permute-done.12 = f32[8,24,128]{2,1,0:T(8,128)S(1)} collective-permute-done((f32[8,24,128]{2,1,0:T(8,128)}, f32[8,24,128]{2,1,0:T(8,128)S(1)}, u32[]{:S(2)}, u32[]{:S(2)}) %collective-permute-start.12) | collective-permute-done | bytes 98336 | tf_op jit(solution)/shard_map/ppermute | solution.py:169
  48.0 0.9 %slice_add_fusion.3 = (f32[4,24,128]{2,1,0:T(8,128)S(1)}, f32[4,24,128]{2,1,0:T(8,128)S(1)}) fusion(f32[8,24,128]{2,1,0:T(8,128)S(1)} %collective-permute-done.12, f32[8,24,128]{2,1,0:T(8,128)} %get-tuple-element.8), kind=kLoop, calls=%fused_computation.9 | loop fusion | flops 24576 | bytes 294912 | tf_op jit(solution)/shard_map/add | solution.py:171
  49.0 4.1 %collective-permute-done.13 = f32[4,24,128]{2,1,0:T(8,128)S(1)} collective-permute-done((f32[4,24,128]{2,1,0:T(8,128)S(1)}, f32[4,24,128]{2,1,0:T(8,128)S(1)}, u32[]{:S(2)}, u32[]{:S(2)}) %collective-permute-start.13) | collective-permute-done | bytes 49184 | tf_op jit(solution)/shard_map/ppermute | solution.py:169
  53.0 4.3 %collective-permute-start.14 = (f32[2,24,128]{2,1,0:T(8,128)S(1)}, f32[2,24,128]{2,1,0:T(8,128)S(1)}, u32[]{:S(2)}, u32[]{:S(2)}) collective-permute-start(f32[2,24,128]{2,1,0:T(8,128)S(1)} %get-tuple-element.17), channel_id=1, source_target_pairs={{0,40},{16,56},{4,44},{20,60},{8,32},{24,48},{12,36},{28,52},{32,8... | collective-permute-start | bytes 73736 | tf_op jit(solution)/shard_map/ppermute | solution.py:169
  57.7 1.6 %collective-permute-done.14 = f32[2,24,128]{2,1,0:T(8,128)S(1)} collective-permute-done((f32[2,24,128]{2,1,0:T(8,128)S(1)}, f32[2,24,128]{2,1,0:T(8,128)S(1)}, u32[]{:S(2)}, u32[]{:S(2)}) %collective-permute-start.14) | collective-permute-done | bytes 24608 | tf_op jit(solution)/shard_map/ppermute | solution.py:169
  59.2 2.2 %collective-permute-start.15 = (f32[1,24,128]{2,1,0:T(8,128)S(1)}, f32[1,24,128]{2,1,0:T(8,128)S(1)}, u32[]{:S(2)}, u32[]{:S(2)}) collective-permute-start(f32[1,24,128]{2,1,0:T(8,128)S(1)} %slice_add_fusion.10), channel_id=1, source_target_pairs={{0,8},{16,24},{4,12},{20,28},{8,0},{24,16},{12,4},{28,20},{32,40},... | collective-permute-start | bytes 36872 | tf_op jit(solution)/shard_map/ppermute | solution.py:198
  61.8 2.0 %collective-permute-done.15 = f32[1,24,128]{2,1,0:T(8,128)S(1)} collective-permute-done((f32[1,24,128]{2,1,0:T(8,128)S(1)}, f32[1,24,128]{2,1,0:T(8,128)S(1)}, u32[]{:S(2)}, u32[]{:S(2)}) %collective-permute-start.15) | collective-permute-done | bytes 12320 | tf_op jit(solution)/shard_map/ppermute | solution.py:198
  63.8 2.4 %collective-permute-done.9 = f32[4,48,128]{2,1,0:T(8,128)S(1)} collective-permute-done((f32[4,48,128]{2,1,0:T(8,128)S(1)}, f32[4,48,128]{2,1,0:T(8,128)S(1)}, u32[]{:S(2)}, u32[]{:S(2)}) %collective-permute-start.9) | collective-permute-done | bytes 98336 | tf_op jit(solution)/shard_map/ppermute | solution.py:169
  66.2 2.1 %collective-permute-start.10 = (f32[2,48,128]{2,1,0:T(8,128)S(1)}, f32[2,48,128]{2,1,0:T(8,128)S(1)}, u32[]{:S(2)}, u32[]{:S(2)}) collective-permute-start(f32[2,48,128]{2,1,0:T(8,128)S(1)} %get-tuple-element.15), channel_id=1, source_target_pairs={{0,3},{16,19},{4,7},{20,23},{8,11},{24,27},{12,15},{28,31},{32,35}... | collective-permute-start | bytes 147464 | tf_op jit(solution)/shard_map/ppermute | solution.py:169
  68.4 3.2 %collective-permute-done.10 = f32[2,48,128]{2,1,0:T(8,128)S(1)} collective-permute-done((f32[2,48,128]{2,1,0:T(8,128)S(1)}, f32[2,48,128]{2,1,0:T(8,128)S(1)}, u32[]{:S(2)}, u32[]{:S(2)}) %collective-permute-start.10) | collective-permute-done | bytes 49184 | tf_op jit(solution)/shard_map/ppermute | solution.py:169
  72.2 3.2 %collective-permute-done.11 = f32[1,48,128]{2,1,0:T(8,128)S(1)} collective-permute-done((f32[1,48,128]{2,1,0:T(8,128)S(1)}, f32[1,48,128]{2,1,0:T(8,128)S(1)}, u32[]{:S(2)}, u32[]{:S(2)}) %collective-permute-start.11) | collective-permute-done | bytes 24608 | tf_op jit(solution)/shard_map/ppermute | solution.py:197
  (54 shorter events, 5.8 us)
Async XLA Ops:
  1.4 2.2 %copy-start.6 = (f32[51,64]{1,0:T(8,128)S(1)}, f32[51,64]{1,0:T(8,128)}, u32[]{:S(2)}) copy-start(f32[51,64]{1,0:T(8,128)} %param.4) | copy-start | bytes 39172
  2.1 5.6 %collective-permute-start = (f32[1,51,128]{2,1,0:T(8,128)S(1)}, f32[1,51,128]{2,1,0:T(8,128)S(1)}, u32[]{:S(2)}, u32[]{:S(2)}) collective-permute-start(f32[1,51,128]{2,1,0:T(8,128)S(1)} %maximum_bitcast_fusion), channel_id=1, source_target_pairs={{0,1},{16,17},{4,5},{20,21},{8,9},{24,25},{12,13},{28,29},{32,33},... | collective-permute-start | bytes 78344 | tf_op jit(solution)/shard_map/ppermute | solution.py:165
  4.3 5.5 %collective-permute-start.4 = (f32[1,26,128]{2,1,0:T(8,128)S(1)}, f32[1,26,128]{2,1,0:T(8,128)S(1)}, u32[]{:S(2)}, u32[]{:S(2)}) collective-permute-start(f32[1,26,128]{2,1,0:T(8,128)S(1)} %fusion.4), channel_id=1, source_target_pairs={{0,8},{16,24},{4,12},{20,28},{8,0},{24,16},{12,4},{28,20},{32,40},... | collective-permute-start | bytes 39944 | tf_op jit(solution)/shard_map/ppermute | solution.py:165
  7.7 6.8 %collective-permute-start.1 = (f32[2,51,128]{2,1,0:T(8,128)S(1)}, f32[2,51,128]{2,1,0:T(8,128)S(1)}, u32[]{:S(2)}, u32[]{:S(2)}) collective-permute-start(f32[2,51,128]{2,1,0:T(8,128)S(1)} %pad_maximum_fusion.4), channel_id=1, source_target_pairs={{0,3},{16,19},{4,7},{20,23},{8,11},{24,27},{12,15},{28,31},{32,35}... | collective-permute-start | bytes 156680 | tf_op jit(solution)/shard_map/ppermute | solution.py:165
  9.8 6.6 %collective-permute-start.5 = (f32[2,26,128]{2,1,0:T(8,128)S(1)}, f32[2,26,128]{2,1,0:T(8,128)S(1)}, u32[]{:S(2)}, u32[]{:S(2)}) collective-permute-start(f32[2,26,128]{2,1,0:T(8,128)S(1)} %pad_maximum_fusion.5), channel_id=1, source_target_pairs={{0,40},{16,56},{4,44},{20,60},{8,32},{24,48},{12,36},{28,52},{32,8... | collective-permute-start | bytes 79880 | tf_op jit(solution)/shard_map/ppermute | solution.py:165
  14.4 4.9 %collective-permute-start.2 = (f32[4,51,128]{2,1,0:T(8,128)S(1)}, f32[4,51,128]{2,1,0:T(8,128)S(1)}, u32[]{:S(2)}, u32[]{:S(2)}) collective-permute-start(f32[4,51,128]{2,1,0:T(8,128)S(1)} %pad_maximum_fusion.2), channel_id=1, source_target_pairs={{0,4},{16,20},{4,0},{20,16},{8,12},{24,28},{12,8},{28,24},{32,36},... | collective-permute-start | bytes 313352 | tf_op jit(solution)/shard_map/ppermute | solution.py:165
  16.4 4.3 %collective-permute-start.6 = (f32[4,26,128]{2,1,0:T(8,128)S(1)}, f32[4,26,128]{2,1,0:T(8,128)S(1)}, u32[]{:S(2)}, u32[]{:S(2)}) collective-permute-start(f32[4,26,128]{2,1,0:T(8,128)S(1)} %pad_maximum_fusion.3), channel_id=1, source_target_pairs={{0,64},{16,80},{4,68},{20,84},{8,72},{24,88},{12,76},{28,92},{32,9... | collective-permute-start | bytes 159752 | tf_op jit(solution)/shard_map/ppermute | solution.py:165
  19.3 7.6 %copy-start = (f32[8,51,128]{2,1,0:T(8,128)}, f32[8,51,128]{2,1,0:T(8,128)S(1)}, u32[]{:S(2)}) copy-start(f32[8,51,128]{2,1,0:T(8,128)S(1)} %pad_maximum_fusion.fluid_a) | copy-start | bytes 626692
  19.3 7.6 %collective-permute-start.3 = (f32[8,51,128]{2,1,0:T(8,128)S(1)}, f32[8,51,128]{2,1,0:T(8,128)S(1)}, u32[]{:S(2)}, u32[]{:S(2)}) collective-permute-start(f32[8,51,128]{2,1,0:T(8,128)S(1)} %pad_maximum_fusion.fluid_a), channel_id=1, source_target_pairs={{0,16},{16,0},{4,20},{20,4},{8,24},{24,8},{12,28},{28,12},{32,48},... | collective-permute-start | bytes 626696 | tf_op jit(solution)/shard_map/ppermute | solution.py:165
  20.7 6.3 %copy-start.1 = (f32[8,26,128]{2,1,0:T(8,128)}, f32[8,26,128]{2,1,0:T(8,128)S(1)}, u32[]{:S(2)}) copy-start(f32[8,26,128]{2,1,0:T(8,128)S(1)} %pad_maximum_fusion.1.center_a) | copy-start | bytes 319492
  20.7 6.3 %collective-permute-start.7 = (f32[8,26,128]{2,1,0:T(8,128)S(1)}, f32[8,26,128]{2,1,0:T(8,128)S(1)}, u32[]{:S(2)}, u32[]{:S(2)}) collective-permute-start(f32[8,26,128]{2,1,0:T(8,128)S(1)} %pad_maximum_fusion.1.center_a), channel_id=1, source_target_pairs={{0,192},{16,208},{4,196},{20,212},{8,200},{24,216},{12,204},{28,22... | collective-permute-start | bytes 319496 | tf_op jit(solution)/shard_map/ppermute | solution.py:165
  27.6 0.7 copy-start.2
  41.9 6.0 %collective-permute-start.12 = (f32[8,24,128]{2,1,0:T(8,128)}, f32[8,24,128]{2,1,0:T(8,128)S(1)}, u32[]{:S(2)}, u32[]{:S(2)}) collective-permute-start(f32[8,24,128]{2,1,0:T(8,128)} %get-tuple-element.9), channel_id=1, source_target_pairs={{0,192},{16,208},{4,196},{20,212},{8,200},{24,216},{12,204},{28,22... | collective-permute-start | bytes 294920 | tf_op jit(solution)/shard_map/ppermute | solution.py:169
  48.0 1.0 %copy-start.8 = (f32[48,4]{0,1:T(4,128)S(1)}, f32[48,4]{0,1:T(4,128)}, u32[]{:S(2)}) copy-start(f32[48,4]{0,1:T(4,128)} %param.5) | copy-start | bytes 2308
  48.0 9.4 %copy-start.5 = (f32[51,128]{1,0:T(8,128)S(1)}, f32[51,128]{1,0:T(8,128)}, u32[]{:S(2)}) copy-start(f32[51,128]{1,0:T(8,128)} %param.3) | copy-start | bytes 78340
  48.0 9.6 %copy-start.7 = (f32[8,48,128]{2,1,0:T(8,128)S(1)}, f32[8,48,128]{2,1,0:T(8,128)}, u32[]{:S(2)}) copy-start(f32[8,48,128]{2,1,0:T(8,128)} %get-tuple-element.7) | copy-start | bytes 589828
  48.8 12.6 %copy-start.3 = (f32[8,48,128]{2,1,0:T(8,128)S(1)}, f32[8,48,128]{2,1,0:T(8,128)}, u32[]{:S(2)}) copy-start(f32[8,48,128]{2,1,0:T(8,128)} %get-tuple-element.6) | copy-start | bytes 589828
  48.8 4.2 %collective-permute-start.13 = (f32[4,24,128]{2,1,0:T(8,128)S(1)}, f32[4,24,128]{2,1,0:T(8,128)S(1)}, u32[]{:S(2)}, u32[]{:S(2)}) collective-permute-start(f32[4,24,128]{2,1,0:T(8,128)S(1)} %get-tuple-element.13), channel_id=1, source_target_pairs={{0,64},{16,80},{4,68},{20,84},{8,72},{24,88},{12,76},{28,92},{32,9... | collective-permute-start | bytes 147464 | tf_op jit(solution)/shard_map/ppermute | solution.py:169
  53.0 6.2 %collective-permute-start.14 = (f32[2,24,128]{2,1,0:T(8,128)S(1)}, f32[2,24,128]{2,1,0:T(8,128)S(1)}, u32[]{:S(2)}, u32[]{:S(2)}) collective-permute-start(f32[2,24,128]{2,1,0:T(8,128)S(1)} %get-tuple-element.17), channel_id=1, source_target_pairs={{0,40},{16,56},{4,44},{20,60},{8,32},{24,48},{12,36},{28,52},{32,8... | collective-permute-start | bytes 73736 | tf_op jit(solution)/shard_map/ppermute | solution.py:169
  57.6 3.9 %collective-permute-start.8 = (f32[8,48,128]{2,1,0:T(8,128)S(1)}, f32[8,48,128]{2,1,0:T(8,128)S(1)}, u32[]{:S(2)}, u32[]{:S(2)}) collective-permute-start(f32[8,48,128]{2,1,0:T(8,128)S(1)} %copy-done.7), channel_id=1, source_target_pairs={{0,16},{16,0},{4,20},{20,4},{8,24},{24,8},{12,28},{28,12},{32,48},... | collective-permute-start | bytes 589832 | tf_op jit(solution)/shard_map/ppermute | solution.py:169
  59.2 4.6 %collective-permute-start.15 = (f32[1,24,128]{2,1,0:T(8,128)S(1)}, f32[1,24,128]{2,1,0:T(8,128)S(1)}, u32[]{:S(2)}, u32[]{:S(2)}) collective-permute-start(f32[1,24,128]{2,1,0:T(8,128)S(1)} %slice_add_fusion.10), channel_id=1, source_target_pairs={{0,8},{16,24},{4,12},{20,28},{8,0},{24,16},{12,4},{28,20},{32,40},... | collective-permute-start | bytes 36872 | tf_op jit(solution)/shard_map/ppermute | solution.py:198
  61.5 4.7 %collective-permute-start.9 = (f32[4,48,128]{2,1,0:T(8,128)S(1)}, f32[4,48,128]{2,1,0:T(8,128)S(1)}, u32[]{:S(2)}, u32[]{:S(2)}) collective-permute-start(f32[4,48,128]{2,1,0:T(8,128)S(1)} %get-tuple-element.11), channel_id=1, source_target_pairs={{0,4},{16,20},{4,0},{20,16},{8,12},{24,28},{12,8},{28,24},{32,36},... | collective-permute-start | bytes 294920 | tf_op jit(solution)/shard_map/ppermute | solution.py:169
  66.2 5.4 %collective-permute-start.10 = (f32[2,48,128]{2,1,0:T(8,128)S(1)}, f32[2,48,128]{2,1,0:T(8,128)S(1)}, u32[]{:S(2)}, u32[]{:S(2)}) collective-permute-start(f32[2,48,128]{2,1,0:T(8,128)S(1)} %get-tuple-element.15), channel_id=1, source_target_pairs={{0,3},{16,19},{4,7},{20,23},{8,11},{24,27},{12,15},{28,31},{32,35}... | collective-permute-start | bytes 147464 | tf_op jit(solution)/shard_map/ppermute | solution.py:169
  71.6 3.8 %collective-permute-start.11 = (f32[1,48,128]{2,1,0:T(8,128)S(1)}, f32[1,48,128]{2,1,0:T(8,128)S(1)}, u32[]{:S(2)}, u32[]{:S(2)}) collective-permute-start(f32[1,48,128]{2,1,0:T(8,128)S(1)} %slice_add_fusion.8), channel_id=1, source_target_pairs={{0,1},{16,17},{4,5},{20,21},{8,9},{24,25},{12,13},{28,29},{32,33},... | collective-permute-start | bytes 73736 | tf_op jit(solution)/shard_map/ppermute | solution.py:197
  (3 other events, 2.0 us)

commit v3 on v2

--- a/solution.py
+++ b/solution.py
@@ -5,11 +5,13 @@
 from jax.experimental.pallas import tpu as pltpu
 from jax.sharding import PartitionSpec as P
 
+
 WAVES = 64
 COLS = 48
 LANES = 128
 LEAD = -1.9530316595457846
 TAIL = (-3.3578779781881196, 6.240606194702548, -6.649373004251278, 3.3689630874951395, -0.5120242670059871)
+
 
 def tile_values(cx, cy, cz, fx, fy, fz):
     dx = cx - fx
@@ -25,24 +27,25 @@
         p = p * z + c
     return (rest * inv) * p
 
+
 def split(a):
     hi = a.astype(jnp.bfloat16)
     lo = (a - hi.astype(jnp.float32)).astype(jnp.bfloat16)
     return hi, lo
+
 
 def coupling_body(fluid_a, fluid_b, center_a, center_b, motion_a, motion_b, load_a, load_b, cpos, cval, fval, fpos, t0, t1, acc, loads):
     hf = fluid_a.shape[0]
     nf = 2 * hf
     hb = center_a.shape[0] // 2
     nb = 2 * hb
-    width = nf * LANES
     half = lax.broadcasted_iota(jnp.int32, (1, LANES), 1) < LANES // 2
     for k in range(nf):
         chunk = (fluid_a, fluid_b)[k // hf].at[k % hf]
-        hi, lo = split(chunk[0:COLS, :] * LEAD)
+        hi, lo = split(chunk[3:3 + COLS, :] * LEAD)
         fval[0:COLS, k * LANES:(k + 1) * LANES] = hi
         fval[COLS:2 * COLS, k * LANES:(k + 1) * LANES] = lo
-        fpos[:, k * LANES:(k + 1) * LANES] = chunk[COLS:COLS + 3, :] * float(WAVES)
+        fpos[:, k * LANES:(k + 1) * LANES] = chunk[0:3, :] * float(WAVES)
     for b in range(nb):
         side = (center_a, center_b)[b // hb]
         one = side[2 * (b % hb)]
@@ -78,12 +81,14 @@
         loads[pl.ds(b * LANES, LANES), :] = back[0:LANES, :] + back[LANES:2 * LANES, :]
 
     compute(0, t0)
+
     def pair(p, c):
         compute(2 * p + 1, t1)
         dots(2 * p, t0)
         compute(2 * p + 2, t0)
         dots(2 * p + 1, t1)
         return c
+
     lax.fori_loop(0, nb // 2 - 1, pair, 0)
     compute(nb - 1, t1)
     dots(nb - 2, t0)
@@ -100,6 +105,7 @@
         side = (load_a, load_b)[b // hb]
         side[2 * (b % hb)] = jnp.where(half, top, pltpu.roll(bot, LANES // 2, 1))
         side[2 * (b % hb) + 1] = jnp.where(half, pltpu.roll(top, LANES // 2, 1), bot)
+
 
 def coupling(fluid_a, fluid_b, center_a, center_b):
     hf = fluid_a.shape[0]
@@ -123,8 +129,29 @@
             pltpu.VMEM((2 * COLS, width), jnp.float32),
             pltpu.VMEM((nb * LANES, 2 * COLS), jnp.float32),
         ],
+        compiler_params=pltpu.CompilerParams(vmem_limit_bytes=16 * 2**20),
         name="coupling",
     )(fluid_a, fluid_b, center_a, center_b)
+
+
+def pack_body(center, out):
+    half = center.shape[1]
+    out[0:24, 0:half] = center[3:27, :]
+    out[0:24, half:] = center[27:51, :]
+    out[24:26, 0:half] = center[0:2, :]
+    out[24:25, half:] = center[2:3, :]
+    out[25:26, half:] = jnp.zeros((1, half), jnp.float32)
+
+
+def packed(center):
+    return pl.pallas_call(
+        pack_body,
+        out_shape=jax.ShapeDtypeStruct((26, LANES), jnp.float32),
+        in_specs=[pl.BlockSpec(memory_space=pltpu.VMEM)],
+        out_specs=pl.BlockSpec(memory_space=pltpu.VMEM),
+        compiler_params=pltpu.CompilerParams(vmem_limit_bytes=2**20),
+        name="pack",
+    )(center)
 
 
 AXES = ("row", "col")
@@ -172,17 +199,8 @@
 
 
 def per_device(fluid_data, center_data, poly_coef):
-    fluid = jnp.concatenate([fluid_data[3:], fluid_data[:3]], 0)
-    places = jnp.concatenate([center_data[0:2], center_data[2:3], jnp.zeros_like(center_data[:1])], 0)
-    center = jnp.concatenate(
-        [
-            jnp.concatenate([center_data[3:27], center_data[27:51]], 1),
-            jnp.concatenate([places[0:2], places[2:4]], 1),
-        ],
-        0,
-    )
-    fluid = fluid[None]
-    center = center[None]
+    fluid = fluid_data[None]
+    center = packed(center_data)[None]
     fluids = (fluid, None)
     centers = (center, None)
     for i in range(4):
@@ -192,10 +210,10 @@
         centers = gather_step(held, CENTER_STAGES[i])
     motion, motion_away, loads, loads_away = coupling(*fluids, *centers)
     for i in (3, 2, 1):
+        loads, loads_away = sum_step(loads, loads_away, CENTER_STAGES[i])
         motion, motion_away = sum_step(motion, motion_away, FLUID_STAGES[i])
-        loads, loads_away = sum_step(loads, loads_away, CENTER_STAGES[i])
+    loads = (loads + lax.ppermute(loads_away, AXES, CENTER_STAGES[0]))[0]
     motion = (motion + lax.ppermute(motion_away, AXES, FLUID_STAGES[0]))[0]
-    loads = (loads + lax.ppermute(loads_away, AXES, CENTER_STAGES[0]))[0]
     affine = poly_coef[:, 0:1] + jnp.dot(
         poly_coef[:, 1:],
         fluid_data[:3],

time: 76.4 us -> 70.7 us (0.925)
  local copies, waits for them, and re-layouts: 3.54 us -> 1.39 us
  Pallas kernels: 13.6 us -> 11.8 us
  other arithmetic: 2.3 us -> 1.36 us
    slice x7 -> x0, local copies, waits for them, and re-layouts: 2.12 us -> none  [the longest x3 1.43 us: per_device(): fluid = jnp.concatenate([fluid_data[3:], fluid_data[:3]], 0)]
    pallas_call x1, Pallas kernels: 13.6 us -> 11.7 us  [coupling(): pl.pallas_call(coupling_body, out_shape=(motion, motion, load, load), in_...]
    add x6, other arithmetic: 0.93 us -> 0.07 us  [sum_step(): return (mine[:half] + arrived[:half], mine[half:] + arrived[half:])]
where the time goes in v3:
time: 70.7 us; the launch traced here: 70.4 us
  starting transfers between devices  29.5 us (42%)
  waiting for transfers between devices  25.5 us (36%)
  Pallas kernels  11.8 us (17%)
  local copies, waits for them, and re-layouts  1.39 us (2%)
  other arithmetic  1.36 us (2%)
  between operations  0.71 us (1%)
    ppermute x8, starting transfers between devices, gather_step(): return (held, lax.ppermute(held, AXES, stage))  17.5 us
    ppermute x6, waiting for transfers between devices, sum_step(): arrived = lax.ppermute(theirs, AXES, stage)  13.6 us
    pallas_call x1, Pallas kernels, coupling(): pl.pallas_call(coupling_body, out_shape=(motion, motion, load, load), in_...  11.7 us
    ppermute x6, starting transfers between devices, sum_step(): arrived = lax.ppermute(theirs, AXES, stage)  9.67 us
    ppermute x8, waiting for transfers between devices, gather_step(): return (held, lax.ppermute(held, AXES, stage))  6.63 us
    ppermute x1, waiting for transfers between devices, per_device(): motion = (motion + lax.ppermute(motion_away, AXES, FLUID_STAGES[0]))[0]  3.21 us
    ppermute x1, starting transfers between devices, per_device(): loads = (loads + lax.ppermute(loads_away, AXES, CENTER_STAGES[0]))[0]  2.24 us
    ppermute x1, waiting for transfers between devices, per_device(): loads = (loads + lax.ppermute(loads_away, AXES, CENTER_STAGES[0]))[0]  2.04 us
  transfers between devices with their start and end apart: 16, of which 11 were waited for; matrix products, arithmetic and copies ran while one was open for 1% of the time, Pallas kernels for 0%

profile of v3, /device:TPU:32, one launch (start us, length us, event | category | flops | bytes accessed | tf_op | source)
XLA Modules:
  0.0 70.4 jit_solution(16646377494151088769)
XLA Ops:
  0.6 1.6 %collective-permute-start = (f32[1,51,128]{2,1,0:T(8,128)}, f32[1,51,128]{2,1,0:T(8,128)S(1)}, u32[]{:S(2)}, u32[]{:S(2)}) collective-permute-start(f32[1,51,128]{2,1,0:T(8,128)} %bitcast.14), channel_id=1, source_target_pairs={{0,1},{16,17},{4,5},{20,21},{8,9},{24,25},{12,13},{28,29},{32,33},... | collective-permute-start | bytes 78344 | tf_op jit(solution)/shard_map/ppermute | solution.py:192
  2.2 0.7 %copy-done = f32[51,64]{1,0:T(8,128)S(1)} copy-done((f32[51,64]{1,0:T(8,128)S(1)}, f32[51,64]{1,0:T(8,128)}, u32[]{:S(2)}) %copy-start) | copy-done | bytes 13080
  3.0 3.3 %collective-permute-start.4 = (f32[1,26,128]{2,1,0:T(8,128)S(1)}, f32[1,26,128]{2,1,0:T(8,128)S(1)}, u32[]{:S(2)}, u32[]{:S(2)}) collective-permute-start(f32[1,26,128]{2,1,0:T(8,128)S(1)} %bitcast.10), channel_id=1, source_target_pairs={{0,8},{16,24},{4,12},{20,28},{8,0},{24,16},{12,4},{28,20},{32,40},... | collective-permute-start | bytes 39944 | tf_op jit(solution)/shard_map/ppermute | solution.py:192
  6.3 2.2 %collective-permute-start.1 = (f32[2,51,128]{2,1,0:T(8,128)S(1)}, f32[2,51,128]{2,1,0:T(8,128)S(1)}, u32[]{:S(2)}, u32[]{:S(2)}) collective-permute-start(f32[2,51,128]{2,1,0:T(8,128)S(1)} %pad_maximum_fusion.4), channel_id=1, source_target_pairs={{0,3},{16,19},{4,7},{20,23},{8,11},{24,27},{12,15},{28,31},{32,35}... | collective-permute-start | bytes 156680 | tf_op jit(solution)/shard_map/ppermute | solution.py:192
  8.5 4.6 %collective-permute-start.5 = (f32[2,26,128]{2,1,0:T(8,128)S(1)}, f32[2,26,128]{2,1,0:T(8,128)S(1)}, u32[]{:S(2)}, u32[]{:S(2)}) collective-permute-start(f32[2,26,128]{2,1,0:T(8,128)S(1)} %pad_maximum_fusion.5), channel_id=1, source_target_pairs={{0,40},{16,56},{4,44},{20,60},{8,32},{24,48},{12,36},{28,52},{32,8... | collective-permute-start | bytes 79880 | tf_op jit(solution)/shard_map/ppermute | solution.py:192
  13.2 1.1 %collective-permute-start.2 = (f32[4,51,128]{2,1,0:T(8,128)S(1)}, f32[4,51,128]{2,1,0:T(8,128)S(1)}, u32[]{:S(2)}, u32[]{:S(2)}) collective-permute-start(f32[4,51,128]{2,1,0:T(8,128)S(1)} %pad_maximum_fusion.2), channel_id=1, source_target_pairs={{0,4},{16,20},{4,0},{20,16},{8,12},{24,28},{12,8},{28,24},{32,36},... | collective-permute-start | bytes 313352 | tf_op jit(solution)/shard_map/ppermute | solution.py:192
  14.3 0.9 %collective-permute-done.5 = f32[2,26,128]{2,1,0:T(8,128)S(1)} collective-permute-done((f32[2,26,128]{2,1,0:T(8,128)S(1)}, f32[2,26,128]{2,1,0:T(8,128)S(1)}, u32[]{:S(2)}, u32[]{:S(2)}) %collective-permute-start.5) | collective-permute-done | bytes 26656 | tf_op jit(solution)/shard_map/ppermute | solution.py:192
  15.2 1.6 %collective-permute-start.6 = (f32[4,26,128]{2,1,0:T(8,128)S(1)}, f32[4,26,128]{2,1,0:T(8,128)S(1)}, u32[]{:S(2)}, u32[]{:S(2)}) collective-permute-start(f32[4,26,128]{2,1,0:T(8,128)S(1)} %pad_maximum_fusion.3), channel_id=1, source_target_pairs={{0,64},{16,80},{4,68},{20,84},{8,72},{24,88},{12,76},{28,92},{32,9... | collective-permute-start | bytes 159752 | tf_op jit(solution)/shard_map/ppermute | solution.py:192
  16.7 1.3 %collective-permute-done.2 = f32[4,51,128]{2,1,0:T(8,128)S(1)} collective-permute-done((f32[4,51,128]{2,1,0:T(8,128)S(1)}, f32[4,51,128]{2,1,0:T(8,128)S(1)}, u32[]{:S(2)}, u32[]{:S(2)}) %collective-permute-start.2) | collective-permute-done | bytes 104480 | tf_op jit(solution)/shard_map/ppermute | solution.py:192
  18.2 1.3 %collective-permute-done.6 = f32[4,26,128]{2,1,0:T(8,128)S(1)} collective-permute-done((f32[4,26,128]{2,1,0:T(8,128)S(1)}, f32[4,26,128]{2,1,0:T(8,128)S(1)}, u32[]{:S(2)}, u32[]{:S(2)}) %collective-permute-start.6) | collective-permute-done | bytes 53280 | tf_op jit(solution)/shard_map/ppermute | solution.py:192
  19.4 3.1 %collective-permute-start.7 = (f32[8,26,128]{2,1,0:T(8,128)S(1)}, f32[8,26,128]{2,1,0:T(8,128)S(1)}, u32[]{:S(2)}, u32[]{:S(2)}) collective-permute-start(f32[8,26,128]{2,1,0:T(8,128)S(1)} %pad_maximum_fusion.1.center_a), channel_id=1, source_target_pairs={{0,192},{16,208},{4,196},{20,212},{8,200},{24,216},{12,204},{28,22... | collective-permute-start | bytes 319496 | tf_op jit(solution)/shard_map/ppermute | solution.py:192
  22.5 3.2 %collective-permute-done.7.center_b = f32[8,26,128]{2,1,0:T(8,128)S(1)} collective-permute-done((f32[8,26,128]{2,1,0:T(8,128)S(1)}, f32[8,26,128]{2,1,0:T(8,128)S(1)}, u32[]{:S(2)}, u32[]{:S(2)}) %collective-permute-start.7) | collective-permute-done | bytes 106528 | tf_op jit(solution)/shard_map/ppermute | solution.py:192
  25.7 11.7 %coupling.1 = (f32[8,48,128]{2,1,0:T(8,128)S(1)}, f32[8,48,128]{2,1,0:T(8,128)S(1)}, f32[8,24,128]{2,1,0:T(8,128)S(1)}, f32[8,24,128]{2,1,0:T(8,128)S(1)}) custom-call(f32[8,51,128]{2,1,0:T(8,128)S(1)} %pad_maximum_fusion.fluid_a, f32[8,51,128]{2,1,0:T(8,128)S(1)} %collective-permute-done.3.fluid_b, f32[8,26,128]{2,1,0:T(8,128)S(1)} %pad_maximum_fusion.1.center_a, ...), custom_call_target="tpu_custom_call" | custom-call | tf_op jit(solution)/shard_map/coupling/pallas_call | solution.py:117
  37.4 3.1 %collective-permute-start.12 = (f32[8,24,128]{2,1,0:T(8,128)S(1)}, f32[8,24,128]{2,1,0:T(8,128)S(1)}, u32[]{:S(2)}, u32[]{:S(2)}) collective-permute-start(f32[8,24,128]{2,1,0:T(8,128)S(1)} %get-tuple-element.9), channel_id=1, source_target_pairs={{0,192},{16,208},{4,196},{20,212},{8,200},{24,216},{12,204},{28,22... | collective-permute-start | bytes 294920 | tf_op jit(solution)/shard_map/ppermute | solution.py:196
  40.5 2.8 %collective-permute-done.12 = f32[8,24,128]{2,1,0:T(8,128)S(1)} collective-permute-done((f32[8,24,128]{2,1,0:T(8,128)S(1)}, f32[8,24,128]{2,1,0:T(8,128)S(1)}, u32[]{:S(2)}, u32[]{:S(2)}) %collective-permute-start.12) | collective-permute-done | bytes 98336 | tf_op jit(solution)/shard_map/ppermute | solution.py:196
  44.0 3.5 %collective-permute-done.13 = f32[4,24,128]{2,1,0:T(8,128)S(1)} collective-permute-done((f32[4,24,128]{2,1,0:T(8,128)S(1)}, f32[4,24,128]{2,1,0:T(8,128)S(1)}, u32[]{:S(2)}, u32[]{:S(2)}) %collective-permute-start.13) | collective-permute-done | bytes 49184 | tf_op jit(solution)/shard_map/ppermute | solution.py:196
  47.6 4.1 %collective-permute-start.14 = (f32[2,24,128]{2,1,0:T(8,128)S(1)}, f32[2,24,128]{2,1,0:T(8,128)S(1)}, u32[]{:S(2)}, u32[]{:S(2)}) collective-permute-start(f32[2,24,128]{2,1,0:T(8,128)S(1)} %get-tuple-element.17), channel_id=1, source_target_pairs={{0,40},{16,56},{4,44},{20,60},{8,32},{24,48},{12,36},{28,52},{32,8... | collective-permute-start | bytes 73736 | tf_op jit(solution)/shard_map/ppermute | solution.py:196
  52.2 1.4 %collective-permute-done.14 = f32[2,24,128]{2,1,0:T(8,128)S(1)} collective-permute-done((f32[2,24,128]{2,1,0:T(8,128)S(1)}, f32[2,24,128]{2,1,0:T(8,128)S(1)}, u32[]{:S(2)}, u32[]{:S(2)}) %collective-permute-start.14) | collective-permute-done | bytes 24608 | tf_op jit(solution)/shard_map/ppermute | solution.py:196
  53.6 2.2 %collective-permute-start.15 = (f32[1,24,128]{2,1,0:T(8,128)S(1)}, f32[1,24,128]{2,1,0:T(8,128)S(1)}, u32[]{:S(2)}, u32[]{:S(2)}) collective-permute-start(f32[1,24,128]{2,1,0:T(8,128)S(1)} %slice_add_fusion.10), channel_id=1, source_target_pairs={{0,8},{16,24},{4,12},{20,28},{8,0},{24,16},{12,4},{28,20},{32,40},... | collective-permute-start | bytes 36872 | tf_op jit(solution)/shard_map/ppermute | solution.py:215
  56.2 2.0 %collective-permute-done.15 = f32[1,24,128]{2,1,0:T(8,128)S(1)} collective-permute-done((f32[1,24,128]{2,1,0:T(8,128)S(1)}, f32[1,24,128]{2,1,0:T(8,128)S(1)}, u32[]{:S(2)}, u32[]{:S(2)}) %collective-permute-start.15) | collective-permute-done | bytes 12320 | tf_op jit(solution)/shard_map/ppermute | solution.py:215
  58.2 2.3 %collective-permute-done.9 = f32[4,48,128]{2,1,0:T(8,128)S(1)} collective-permute-done((f32[4,48,128]{2,1,0:T(8,128)S(1)}, f32[4,48,128]{2,1,0:T(8,128)S(1)}, u32[]{:S(2)}, u32[]{:S(2)}) %collective-permute-start.9) | collective-permute-done | bytes 98336 | tf_op jit(solution)/shard_map/ppermute | solution.py:196
  60.6 1.8 %collective-permute-start.10 = (f32[2,48,128]{2,1,0:T(8,128)S(1)}, f32[2,48,128]{2,1,0:T(8,128)S(1)}, u32[]{:S(2)}, u32[]{:S(2)}) collective-permute-start(f32[2,48,128]{2,1,0:T(8,128)S(1)} %get-tuple-element.15), channel_id=1, source_target_pairs={{0,3},{16,19},{4,7},{20,23},{8,11},{24,27},{12,15},{28,31},{32,35}... | collective-permute-start | bytes 147464 | tf_op jit(solution)/shard_map/ppermute | solution.py:196
  62.4 3.5 %collective-permute-done.10 = f32[2,48,128]{2,1,0:T(8,128)S(1)} collective-permute-done((f32[2,48,128]{2,1,0:T(8,128)S(1)}, f32[2,48,128]{2,1,0:T(8,128)S(1)}, u32[]{:S(2)}, u32[]{:S(2)}) %collective-permute-start.10) | collective-permute-done | bytes 49184 | tf_op jit(solution)/shard_map/ppermute | solution.py:196
  66.6 3.2 %collective-permute-done.11 = f32[1,48,128]{2,1,0:T(8,128)S(1)} collective-permute-done((f32[1,48,128]{2,1,0:T(8,128)S(1)}, f32[1,48,128]{2,1,0:T(8,128)S(1)}, u32[]{:S(2)}, u32[]{:S(2)}) %collective-permute-start.11) | collective-permute-done | bytes 24608 | tf_op jit(solution)/shard_map/ppermute | solution.py:216
  (34 shorter events, 3.1 us)
Async XLA Ops:
  0.6 5.7 %collective-permute-start = (f32[1,51,128]{2,1,0:T(8,128)}, f32[1,51,128]{2,1,0:T(8,128)S(1)}, u32[]{:S(2)}, u32[]{:S(2)}) collective-permute-start(f32[1,51,128]{2,1,0:T(8,128)} %bitcast.14), channel_id=1, source_target_pairs={{0,1},{16,17},{4,5},{20,21},{8,9},{24,25},{12,13},{28,29},{32,33},... | collective-permute-start | bytes 78344 | tf_op jit(solution)/shard_map/ppermute | solution.py:192
  2.2 0.7 %copy-start = (f32[51,64]{1,0:T(8,128)S(1)}, f32[51,64]{1,0:T(8,128)}, u32[]{:S(2)}) copy-start(f32[51,64]{1,0:T(8,128)} %center.1) | copy-start | bytes 39172
  3.0 3.4 %copy-start.1 = (f32[51,128]{1,0:T(8,128)S(1)}, f32[51,128]{1,0:T(8,128)}, u32[]{:S(2)}) copy-start(f32[51,128]{1,0:T(8,128)} %param.3) | copy-start | bytes 78340
  3.0 5.5 %collective-permute-start.4 = (f32[1,26,128]{2,1,0:T(8,128)S(1)}, f32[1,26,128]{2,1,0:T(8,128)S(1)}, u32[]{:S(2)}, u32[]{:S(2)}) collective-permute-start(f32[1,26,128]{2,1,0:T(8,128)S(1)} %bitcast.10), channel_id=1, source_target_pairs={{0,8},{16,24},{4,12},{20,28},{8,0},{24,16},{12,4},{28,20},{32,40},... | collective-permute-start | bytes 39944 | tf_op jit(solution)/shard_map/ppermute | solution.py:192
  6.3 6.8 %collective-permute-start.1 = (f32[2,51,128]{2,1,0:T(8,128)S(1)}, f32[2,51,128]{2,1,0:T(8,128)S(1)}, u32[]{:S(2)}, u32[]{:S(2)}) collective-permute-start(f32[2,51,128]{2,1,0:T(8,128)S(1)} %pad_maximum_fusion.4), channel_id=1, source_target_pairs={{0,3},{16,19},{4,7},{20,23},{8,11},{24,27},{12,15},{28,31},{32,35}... | collective-permute-start | bytes 156680 | tf_op jit(solution)/shard_map/ppermute | solution.py:192
  8.5 6.6 %collective-permute-start.5 = (f32[2,26,128]{2,1,0:T(8,128)S(1)}, f32[2,26,128]{2,1,0:T(8,128)S(1)}, u32[]{:S(2)}, u32[]{:S(2)}) collective-permute-start(f32[2,26,128]{2,1,0:T(8,128)S(1)} %pad_maximum_fusion.5), channel_id=1, source_target_pairs={{0,40},{16,56},{4,44},{20,60},{8,32},{24,48},{12,36},{28,52},{32,8... | collective-permute-start | bytes 79880 | tf_op jit(solution)/shard_map/ppermute | solution.py:192
  13.2 4.9 %collective-permute-start.2 = (f32[4,51,128]{2,1,0:T(8,128)S(1)}, f32[4,51,128]{2,1,0:T(8,128)S(1)}, u32[]{:S(2)}, u32[]{:S(2)}) collective-permute-start(f32[4,51,128]{2,1,0:T(8,128)S(1)} %pad_maximum_fusion.2), channel_id=1, source_target_pairs={{0,4},{16,20},{4,0},{20,16},{8,12},{24,28},{12,8},{28,24},{32,36},... | collective-permute-start | bytes 313352 | tf_op jit(solution)/shard_map/ppermute | solution.py:192
  15.2 4.3 %collective-permute-start.6 = (f32[4,26,128]{2,1,0:T(8,128)S(1)}, f32[4,26,128]{2,1,0:T(8,128)S(1)}, u32[]{:S(2)}, u32[]{:S(2)}) collective-permute-start(f32[4,26,128]{2,1,0:T(8,128)S(1)} %pad_maximum_fusion.3), channel_id=1, source_target_pairs={{0,64},{16,80},{4,68},{20,84},{8,72},{24,88},{12,76},{28,92},{32,9... | collective-permute-start | bytes 159752 | tf_op jit(solution)/shard_map/ppermute | solution.py:192
  18.1 7.6 %collective-permute-start.3 = (f32[8,51,128]{2,1,0:T(8,128)S(1)}, f32[8,51,128]{2,1,0:T(8,128)S(1)}, u32[]{:S(2)}, u32[]{:S(2)}) collective-permute-start(f32[8,51,128]{2,1,0:T(8,128)S(1)} %pad_maximum_fusion.fluid_a), channel_id=1, source_target_pairs={{0,16},{16,0},{4,20},{20,4},{8,24},{24,8},{12,28},{28,12},{32,48},... | collective-permute-start | bytes 626696 | tf_op jit(solution)/shard_map/ppermute | solution.py:192
  19.4 6.3 %collective-permute-start.7 = (f32[8,26,128]{2,1,0:T(8,128)S(1)}, f32[8,26,128]{2,1,0:T(8,128)S(1)}, u32[]{:S(2)}, u32[]{:S(2)}) collective-permute-start(f32[8,26,128]{2,1,0:T(8,128)S(1)} %pad_maximum_fusion.1.center_a), channel_id=1, source_target_pairs={{0,192},{16,208},{4,196},{20,212},{8,200},{24,216},{12,204},{28,22... | collective-permute-start | bytes 319496 | tf_op jit(solution)/shard_map/ppermute | solution.py:192
  37.4 5.9 %collective-permute-start.12 = (f32[8,24,128]{2,1,0:T(8,128)S(1)}, f32[8,24,128]{2,1,0:T(8,128)S(1)}, u32[]{:S(2)}, u32[]{:S(2)}) collective-permute-start(f32[8,24,128]{2,1,0:T(8,128)S(1)} %get-tuple-element.9), channel_id=1, source_target_pairs={{0,192},{16,208},{4,196},{20,212},{8,200},{24,216},{12,204},{28,22... | collective-permute-start | bytes 294920 | tf_op jit(solution)/shard_map/ppermute | solution.py:196
  43.4 0.7 copy-start.2
  43.4 4.2 %collective-permute-start.13 = (f32[4,24,128]{2,1,0:T(8,128)S(1)}, f32[4,24,128]{2,1,0:T(8,128)S(1)}, u32[]{:S(2)}, u32[]{:S(2)}) collective-permute-start(f32[4,24,128]{2,1,0:T(8,128)S(1)} %get-tuple-element.13), channel_id=1, source_target_pairs={{0,64},{16,80},{4,68},{20,84},{8,72},{24,88},{12,76},{28,92},{32,9... | collective-permute-start | bytes 147464 | tf_op jit(solution)/shard_map/ppermute | solution.py:196
  47.6 6.0 %collective-permute-start.14 = (f32[2,24,128]{2,1,0:T(8,128)S(1)}, f32[2,24,128]{2,1,0:T(8,128)S(1)}, u32[]{:S(2)}, u32[]{:S(2)}) collective-permute-start(f32[2,24,128]{2,1,0:T(8,128)S(1)} %get-tuple-element.17), channel_id=1, source_target_pairs={{0,40},{16,56},{4,44},{20,60},{8,32},{24,48},{12,36},{28,52},{32,8... | collective-permute-start | bytes 73736 | tf_op jit(solution)/shard_map/ppermute | solution.py:196
  51.9 3.9 %collective-permute-start.8 = (f32[8,48,128]{2,1,0:T(8,128)S(1)}, f32[8,48,128]{2,1,0:T(8,128)S(1)}, u32[]{:S(2)}, u32[]{:S(2)}) collective-permute-start(f32[8,48,128]{2,1,0:T(8,128)S(1)} %get-tuple-element.7), channel_id=1, source_target_pairs={{0,16},{16,0},{4,20},{20,4},{8,24},{24,8},{12,28},{28,12},{32,48},... | collective-permute-start | bytes 589832 | tf_op jit(solution)/shard_map/ppermute | solution.py:196
  53.6 4.6 %collective-permute-start.15 = (f32[1,24,128]{2,1,0:T(8,128)S(1)}, f32[1,24,128]{2,1,0:T(8,128)S(1)}, u32[]{:S(2)}, u32[]{:S(2)}) collective-permute-start(f32[1,24,128]{2,1,0:T(8,128)S(1)} %slice_add_fusion.10), channel_id=1, source_target_pairs={{0,8},{16,24},{4,12},{20,28},{8,0},{24,16},{12,4},{28,20},{32,40},... | collective-permute-start | bytes 36872 | tf_op jit(solution)/shard_map/ppermute | solution.py:215
  55.9 4.7 %collective-permute-start.9 = (f32[4,48,128]{2,1,0:T(8,128)S(1)}, f32[4,48,128]{2,1,0:T(8,128)S(1)}, u32[]{:S(2)}, u32[]{:S(2)}) collective-permute-start(f32[4,48,128]{2,1,0:T(8,128)S(1)} %get-tuple-element.11), channel_id=1, source_target_pairs={{0,4},{16,20},{4,0},{20,16},{8,12},{24,28},{12,8},{28,24},{32,36},... | collective-permute-start | bytes 294920 | tf_op jit(solution)/shard_map/ppermute | solution.py:196
  60.6 5.4 %collective-permute-start.10 = (f32[2,48,128]{2,1,0:T(8,128)S(1)}, f32[2,48,128]{2,1,0:T(8,128)S(1)}, u32[]{:S(2)}, u32[]{:S(2)}) collective-permute-start(f32[2,48,128]{2,1,0:T(8,128)S(1)} %get-tuple-element.15), channel_id=1, source_target_pairs={{0,3},{16,19},{4,7},{20,23},{8,11},{24,27},{12,15},{28,31},{32,35}... | collective-permute-start | bytes 147464 | tf_op jit(solution)/shard_map/ppermute | solution.py:196
  66.0 3.8 %collective-permute-start.11 = (f32[1,48,128]{2,1,0:T(8,128)S(1)}, f32[1,48,128]{2,1,0:T(8,128)S(1)}, u32[]{:S(2)}, u32[]{:S(2)}) collective-permute-start(f32[1,48,128]{2,1,0:T(8,128)S(1)} %slice_add_fusion.8), channel_id=1, source_target_pairs={{0,1},{16,17},{4,5},{20,21},{8,9},{24,25},{12,13},{28,29},{32,33},... | collective-permute-start | bytes 73736 | tf_op jit(solution)/shard_map/ppermute | solution.py:216
